TPU v7x, 128 devices: a whole 4x4x4 slice. The times are simulated.
128 devices in a mesh: tp: 16 (over z, y), dp: 8 (over x, core).
Axes of the slice: x: 4, y: 4, z: 4, core: 2. Of those that a mesh axis runs over, the one named last changes fastest.
Arguments:
- w_in: float32 [16, 384, 2688], P(None, None, 'tp')
- w_out: float32 [16, 1920, 384], P(None, 'tp')
- g_in: float32 [8, 16, 384, 2688], P('dp', None, None, 'tp')
- g_out: float32 [8, 16, 1920, 384], P('dp', None, 'tp')
- m_in: bfloat16 [16, 384, 2688], P(None, 'dp', 'tp')
- m_out: bfloat16 [16, 1920, 384], P(None, 'tp', 'dp')
- r_in: float32 [16, 384], P(None, 'dp')
- c_in: float32 [16, 2688], P(None, 'tp')
- r_out: float32 [16, 1920], P(None, 'tp')
- c_out: float32 [16, 384], P(None, 'dp')
- learn_rate: float32 [], replicated
- weight_decay: float32 [], replicated
- beta_two: float32 [], replicated
Outputs:
- output 1: float32 [16, 384, 2688], P(None, None, 'tp')
- output 2: float32 [16, 1920, 384], P(None, 'tp')
- output 3: bfloat16 [16, 384, 2688], P(None, 'dp', 'tp')
- output 4: bfloat16 [16, 1920, 384], P(None, 'tp', 'dp')
- output 5: float32 [16, 384], P(None, 'dp')
- output 6: float32 [16, 2688], P(None, 'tp')
- output 7: float32 [16, 1920], P(None, 'tp')
- output 8: float32 [16, 384], P(None, 'dp')
All inputs are finite; a program needn't handle non-finite values.
Results may differ from a plain program's by a relative error of at most 0.00121556.
Values sent between devices are 32-bit elements.
A program may use at most 1 GiB of HBM per device.

v0:
```python
import jax
import jax.numpy as jnp
from jax import lax
from jax.sharding import PartitionSpec as P


def local_update(weight, grad_rep, moment, row_old, col_old, learn_rate, weight_decay, beta_two, row_axis, col_axis, row_devs, col_devs):
    dp_dim = 1 if row_axis == 'dp' else 2
    grad_part = lax.psum_scatter(grad_rep[0], 'dp', scatter_dimension=dp_dim, tiled=True)
    n_rows = grad_part.shape[1] * row_devs
    n_cols = grad_part.shape[2] * col_devs
    grad_sq = grad_part * grad_part + 1e-30
    row_mean = lax.psum(jnp.sum(grad_sq, axis=2), col_axis) / n_cols
    col_mean = lax.psum(jnp.sum(grad_sq, axis=1), row_axis) / n_rows
    row_new = beta_two * row_old + (1.0 - beta_two) * row_mean
    col_new = beta_two * col_old + (1.0 - beta_two) * col_mean
    row_avg = lax.psum(jnp.sum(row_new, axis=1), row_axis) / n_rows
    second = row_new[:, :, None] * col_new[:, None, :] / row_avg[:, None, None]
    update = grad_part / jnp.sqrt(second)
    total_sq = lax.psum(jnp.sum(update * update, axis=(1, 2)), ('tp', 'dp'))
    rms_val = jnp.sqrt(total_sq / (n_rows * n_cols))
    update = update / jnp.maximum(1.0, rms_val)[:, None, None]
    mom_new = (0.9 * moment.astype(jnp.float32) + 0.1 * update).astype(jnp.bfloat16)
    width = grad_part.shape[dp_dim]
    w_block = lax.dynamic_slice_in_dim(weight, lax.axis_index('dp') * width, width, axis=dp_dim)
    w_block = w_block - learn_rate * mom_new.astype(jnp.float32) - learn_rate * weight_decay * w_block
    w_new = lax.all_gather(w_block, 'dp', axis=dp_dim, tiled=True)
    return w_new, mom_new, row_new, col_new


def solution(mesh):
    tp_devs = mesh.shape['tp']
    dp_devs = mesh.shape['dp']

    def body(w_in, w_out, g_in, g_out, m_in, m_out, r_in, c_in, r_out, c_out, learn_rate, weight_decay, beta_two):
        in_result = local_update(w_in, g_in, m_in, r_in, c_in, learn_rate, weight_decay, beta_two, 'dp', 'tp', dp_devs, tp_devs)
        out_result = local_update(w_out, g_out, m_out, r_out, c_out, learn_rate, weight_decay, beta_two, 'tp', 'dp', tp_devs, dp_devs)
        return (in_result[0], out_result[0], in_result[1], out_result[1], in_result[2], in_result[3], out_result[2], out_result[3])

    in_specs = (P(None, None, 'tp'), P(None, 'tp', None), P('dp', None, None, 'tp'), P('dp', None, 'tp', None), P(None, 'dp', 'tp'), P(None, 'tp', 'dp'), P(None, 'dp'), P(None, 'tp'), P(None, 'tp'), P(None, 'dp'), P(), P(), P())
    out_specs = (P(None, None, 'tp'), P(None, 'tp', None), P(None, 'dp', 'tp'), P(None, 'tp', 'dp'), P(None, 'dp'), P(None, 'tp'), P(None, 'tp'), P(None, 'dp'))
    return jax.shard_map(body, mesh=mesh, in_specs=in_specs, out_specs=out_specs, check_vma=False)
```

profile of v0, /device:TPU:1, one launch (start us, length us, event | category | flops | bytes accessed | tf_op | source)
XLA Modules:
  0.0 349.0 jit_solution(11722450710849439600)
XLA Ops:
  7.2 0.0 copy-start
  7.2 0.0 reduce-scatter.5.cloned.1.call-start
  7.2 3.7 %copy.24 = f32[1,16,120,384]{2,3,1,0:T(8,128)} copy(f32[1,16,120,384]{3,2,1,0:T(8,128)} %param.16) | data formatting | bytes 5898240 | tf_op args[3]
  10.9 0.0 reduce-scatter.5.cloned.1.call-update
  10.9 0.0 reduce-scatter.3.cloned.1.call-start
  11.0 6.1 %copy.22 = f32[1,16,384,168]{3,2,1,0:T(8,128)} copy(f32[1,16,384,168]{2,3,1,0:T(8,128)} %param.15) | data formatting | bytes 8257536 | tf_op args[2]
  17.0 0.0 reduce-scatter.3.cloned.1.call-update
  17.1 0.0 copy-start.2
  17.1 0.0 all-gather.5.cloned.1.call-start
  19.1 0.0 copy-done
  19.1 1.3 constant_dynamic-slice_fusion
  20.4 1.5 copy.28
  21.9 25.4 %reduce-scatter.5.cloned.1.call-done = f32[16,120,48]{1,2,0:T(8,128)} async-done(((f32[16,120,384]{1,2,0:T(8,128)}), f32[16,120,48]{1,2,0:T(8,128)}) %reduce-scatter.5.cloned.1.call-update) | async-done | bytes 368656 | tf_op jit(solution)/shard_map/reduce_scatter | solution.py:9
  47.2 1.8 fusion.2
  49.0 15.5 %psum.60 = f32[16,120]{1,0:T(8,128)S(1)} all-reduce(f32[16,120]{1,0:T(8,128)S(1)} %get-tuple-element.19), channel_id=1, replica_groups=mesh['tp'=16,'dp'=8] {'dp'}, use_global_device_ids=true, to_apply=%region_11.0 | all-reduce | flops 1920 | bytes 15360 | tf_op jit(solution)/shard_map/psum | solution.py:13
  64.6 1.9 fusion.5
  66.5 27.0 %reduce-scatter.3.cloned.1.call-done = f32[16,48,168]{2,1,0:T(8,128)} async-done(((f32[16,384,168]{2,1,0:T(8,128)}), f32[16,48,168]{2,1,0:T(8,128)}) %reduce-scatter.3.cloned.1.call-update) | async-done | bytes 516112 | tf_op jit(solution)/shard_map/reduce_scatter | solution.py:9
  93.5 1.9 fusion
  95.5 60.7 %all-reduce.1 = (f32[16,48]{1,0:T(8,128)}, f32[16]{0:T(128)}, f32[16,48]{1,0:T(8,128)}) all-reduce(f32[16,48]{1,0:T(8,128)} %get-tuple-element.17, f32[16]{0:T(128)} %get-tuple-element.33, f32[16,48]{1,0:T(8,128)} %get-tuple-element.18), channel_id=1, replica_groups=mesh['tp'=16,'dp'=8] {'tp'}, use_global_device_ids=true, to_apply=%region_2.0 | all-reduce | flops 1552 | bytes 12416 | tf_op jit(solution)/shard_map/psum | solution.py:13
  156.2 1.9 fusion.4
  158.1 36.1 %all-reduce.2 = (f32[16]{0:T(128)}, f32[16,168]{1,0:T(8,128)}) all-reduce(f32[16]{0:T(128)} %get-tuple-element.31, f32[16,168]{1,0:T(8,128)S(1)} %get-tuple-element.16), channel_id=1, replica_groups=mesh['tp'=16,'dp'=8] {'dp'}, use_global_device_ids=true, to_apply=%region_6.0 | all-reduce | flops 2704 | bytes 21632 | tf_op jit(solution)/shard_map/psum | solution.py:17
  194.2 0.7 broadcast_multiply_fusion.1
  194.8 0.0 copy-start.7
  194.8 0.7 broadcast_multiply_fusion
  195.5 0.0 copy-start.6
  195.5 0.7 multiply_add_fusion.2
  196.2 0.0 copy-start.3
  196.2 0.7 multiply_add_fusion.3
  197.0 0.0 copy-start.5
  197.0 0.0 copy-done.7
  197.0 2.0 multiply_reduce_fusion
  199.0 0.0 copy-done.6
  199.0 0.0 copy-done.5
  199.0 1.9 multiply_reduce_fusion.1
  200.9 65.1 %all-reduce = (f32[16]{0:T(128)}, f32[16]{0:T(128)}) all-reduce(f32[16]{0:T(128)} %multiply_reduce_fusion, f32[16]{0:T(128)} %multiply_reduce_fusion.1), channel_id=1, replica_groups=mesh['tp'=16,'dp'=8] {'tp','dp'}, use_global_device_ids=true, to_apply=%region_8.0 | all-reduce | flops 32 | bytes 256 | tf_op jit(solution)/shard_map/psum | solution.py:20
  265.9 1.2 sqrt_maximum_fusion
  267.1 0.0 copy-done.2
  267.1 2.1 multiply_subtract_fusion.1
  269.2 0.0 copy-start.1
  269.2 0.0 copy-start.4
  269.2 0.0 copy-start.8
  269.2 0.0 copy-start.9
  269.3 0.0 all-gather.5.cloned.1.call-update
  269.3 0.0 all-gather.3.cloned.1.call-start
  269.3 3.3 constant_dynamic-slice_fusion.1
  272.7 2.8 copy.27
  275.5 0.0 copy-done.3
  275.5 0.0 copy-done.1
  275.5 0.0 copy-done.4
  275.5 0.0 copy-done.8
  275.5 0.0 copy-done.9
  275.5 2.8 multiply_subtract_fusion
  278.3 0.0 all-gather.3.cloned.1.call-update
  278.3 15.3 %all-gather.5.cloned.1.call-done = f32[16,120,384]{1,2,0:T(8,128)} async-done(((f32[16,120,48]{1,2,0:T(8,128)}), f32[16,120,384]{1,2,0:T(8,128)}) %all-gather.5.cloned.1.call-update) | async-done | bytes 2949136 | tf_op jit(solution)/shard_map/all_gather | solution.py:27
  293.7 3.5 copy.26
  297.1 39.4 %all-gather.3.cloned.1.call-done = f32[16,384,168]{2,1,0:T(8,128)} async-done(((f32[16,48,168]{2,1,0:T(8,128)}), f32[16,384,168]{2,1,0:T(8,128)}) %all-gather.3.cloned.1.call-update) | async-done | bytes 4128784 | tf_op jit(solution)/shard_map/all_gather | solution.py:27
  336.5 5.9 %copy.25 = f32[16,384,168]{1,2,0:T(8,128)} copy(f32[16,384,168]{2,1,0:T(8,128)} %all-gather.3.cloned.1.call-done) | data formatting | bytes 8257536
Async XLA Ops:
  7.2 12.0 %copy-start = (f32[16,120,384]{2,1,0:T(8,128)S(1)}, f32[16,120,384]{2,1,0:T(8,128)}, u32[]{:S(2)}) copy-start(f32[16,120,384]{2,1,0:T(8,128)} %param.14) | copy-start | bytes 8847364
  7.2 40.1 %reduce-scatter.5.cloned.1.call-start = ((), (), s32[]{:S(2)}) async-start(), calls=%async_computation.4 | async-start | bytes 3538944 | tf_op jit(solution)/shard_map/reduce_scatter | solution.py:9
  10.9 82.6 %reduce-scatter.3.cloned.1.call-start = ((), (), s32[]{:S(2)}) async-start(), calls=%async_computation.2 | async-start | bytes 7077888 | tf_op jit(solution)/shard_map/reduce_scatter | solution.py:9
  17.1 250.1 %copy-start.2 = (bf16[16,120,48]{1,2,0:T(8,128)(2,1)S(1)}, bf16[16,120,48]{1,2,0:T(8,128)(2,1)}, u32[]{:S(2)}) copy-start(bf16[16,120,48]{1,2,0:T(8,128)(2,1)} %param.18) | copy-start | bytes 552964
  17.1 276.6 %all-gather.5.cloned.1.call-start = ((), (), s32[]{:S(2)}) async-start(), calls=%async_computation.5 | async-start | bytes 3538944 | tf_op jit(solution)/shard_map/all_gather | solution.py:27
  194.8 2.1 copy-start.7
  195.5 3.5 %copy-start.6 = (f32[16]{0:T(128)}, f32[16]{0:T(128)S(1)}, u32[]{:S(2)}) copy-start(f32[16]{0:T(128)S(1)} %broadcast_multiply_fusion) | copy-start | bytes 196
  196.2 79.2 %copy-start.3 = (f32[16,168]{1,0:T(8,128)}, f32[16,168]{1,0:T(8,128)S(1)}, u32[]{:S(2)}) copy-start(f32[16,168]{1,0:T(8,128)S(1)} %multiply_add_fusion.2) | copy-start | bytes 32260
  197.0 2.0 copy-start.5
  269.2 6.2 %copy-start.1 = (bf16[16,48,168]{2,1,0:T(8,128)(2,1)S(1)}, bf16[16,48,168]{2,1,0:T(8,128)(2,1)}, u32[]{:S(2)}) copy-start(bf16[16,48,168]{2,1,0:T(8,128)(2,1)} %param.17) | copy-start | bytes 774148
  269.2 6.2 %copy-start.4 = (f32[16,48]{1,0:T(8,128)S(1)}, f32[16,48]{1,0:T(8,128)}, u32[]{:S(2)}) copy-start(f32[16,48]{1,0:T(8,128)} %get-tuple-element.32) | copy-start | bytes 9220
  269.2 6.2 %copy-start.8 = (f32[16]{0:T(128)S(1)}, f32[16]{0:T(128)}, u32[]{:S(2)}) copy-start(f32[16]{0:T(128)} %copy-done.7) | copy-start | bytes 196
  269.2 6.2 %copy-start.9 = (f32[16]{0:T(128)S(1)}, f32[16]{0:T(128)}, u32[]{:S(2)}) copy-start(f32[16]{0:T(128)} %get-tuple-element.36) | copy-start | bytes 196
  269.3 67.2 %all-gather.3.cloned.1.call-start = ((), (), s32[]{:S(2)}) async-start(), calls=%async_computation.3 | async-start | bytes 7077888 | tf_op jit(solution)/shard_map/all_gather | solution.py:27
Sparse Core Ops, SparseCore 0:
  11.0 36.1 reduce-scatter.4
  49.6 43.8 reduce-scatter.2
  269.4 24.2 all-gather.4
  295.8 40.6 all-gather.2
where the time goes:
time: 350 us; the launch traced here: 349 us
  blocking collectives  177 us (51%)
  waiting for transfers between devices  107 us (31%)
  local copies, waits for them, and re-layouts  28.1 us (8%)
  other arithmetic  20.4 us (6%)
  between operations  15.8 us (5%)
    psum x2, blocking collectives, local_update(): row_mean = lax.psum(jnp.sum(grad_sq, axis=2), col_axis) / n_cols  76.2 us
    psum x1, blocking collectives, local_update(): total_sq = lax.psum(jnp.sum(update * update, axis=(1, 2)), ('tp', 'dp'))  65.1 us
    all_gather x2, waiting for transfers between devices, local_update(): w_new = lax.all_gather(w_block, 'dp', axis=dp_dim, tiled=True)  54.7 us
    reduce_scatter x2, waiting for transfers between devices, local_update(): lax.psum_scatter(grad_rep[0], 'dp', scatter_dimension=dp_dim, tiled=True)  52.4 us
    psum x1, blocking collectives, local_update(): row_avg = lax.psum(jnp.sum(row_new, axis=1), row_axis) / n_rows  36.1 us
    unnamed x26, local copies, waits for them, and re-layouts  23.5 us
  transfers between devices with their start and end apart: 4, of which 4 were waited for; matrix products, arithmetic and copies ran while one was open for 7% of the time, Pallas kernels for 0%

commit v1 on v0

v1 whole, which is shorter than its diff:
```python
import jax
import jax.numpy as jnp
from jax import lax
from jax.experimental import pallas as pl
from jax.experimental.pallas import tpu as pltpu
from jax.sharding import PartitionSpec as P

F32, BF16 = jnp.float32, jnp.bfloat16
MESH = pl.DeviceIdType.MESH
RING = 4
L, D = 16, 384
KI, NO = 168, 120
LC, LG, NG = 8, 4, 2
Q, LN, B48, B96 = 72, 128, 48, 96
CH, HEAD, MID = 3 * Q, KI - 2 * Q, 256
NI, KIN, NOUT, KO = 384.0, 2688.0, 1920.0, 384.0
KINDS = RV, LY, LZ, SY, SZ, SX = range(6)
OB, OC = 2, 4


def roll(val, shift):
    return pltpu.roll(val, shift % LN, 1)


def lane_of(shape):
    return lax.broadcasted_iota(jnp.int32, shape, 1)


def row_of(shape):
    return lax.broadcasted_iota(jnp.int32, shape, 0)


def colsum(val):
    return jnp.sum(val, axis=0, keepdims=True)


def rowsum(val):
    return jnp.sum(val, axis=1, keepdims=True)


def pick(cond, val):
    return jnp.where(cond, val, 0.0)


def first(num):
    return pl.ds(0, num)


def block(i):
    return pl.ds(Q * i, Q)


def tile_cols(t):
    return pl.ds(LN * t, LN)


def last_quarter(parts):
    lane = lane_of(parts[0].shape)
    tail = jnp.where(lane < 64, roll(parts[1], 64), roll(parts[2], B96))
    return jnp.where(lane < 32, roll(parts[0], 32), tail)


def join_quarters(quarters, keep):
    return [jnp.where(keep, quarters[i], roll(quarters[3], B96 - 32 * i)) for i in range(3)]


def kernel(rate_ref, wd_ref, beta_ref, w_in, w_out, g_in, g_out, m_in, m_out, r_in, c_in, r_out, c_out,
           wn_in, wn_out, mn_in, mn_out, rn_in, cn_in, rn_out, cn_out,
           gbuf, pbuf, pack, via, rin, fin, mall, mraw_in, mraw_out, msend, mt, mpack, tall,
           rvacc, lvacc, lraw, craw, oraw, pads, lvold, rvold, lvnew, rvnew, box_rv, box_ly, box_lz, box_sy, box_sz, box_sx,
           gl_sem, gs_sem, gr_sem, ml_sem, ms_sem, mr_sem, s_sem, via_sem, rin_sem, ags_sem, agr_sem,
           shs_sem, shr_sem, sts_sem, str_sem, vs_sem, vr_sem, ol_sem, os_sem, or_sem, wl_sem):
    tp, dp = lax.axis_index('tp'), lax.axis_index('dp')
    z, y, x, c = tp // RING, tp % RING, dp // 2, dp % 2
    other = 1 - c
    base, pbase = c * LC, other * LC

    def at_x(xx):
        return {'dp': (xx % RING) * 2 + c}

    def at_y(yy):
        return {'tp': z * RING + yy % RING}

    def at_z(zz):
        return {'tp': (zz % RING) * RING + y}

    partner = {'dp': x * 2 + other}

    def local(src, dst, sem):
        return pltpu.make_async_copy(src, dst, sem)

    def remote(src, dst, send_sem, recv_sem, device):
        return pltpu.make_async_remote_copy(src_ref=src, dst_ref=dst, send_sem=send_sem, recv_sem=recv_sem,
                                            device_id=device, device_id_type=MESH)

    barrier = pltpu.get_barrier_semaphore()
    peers = [partner]
    for k in range(1, RING):
        peers += [at_x(x + k), at_y(y + k), at_z(z + k)]
    for peer in peers:
        pl.semaphore_signal(barrier, inc=1, device_id=peer, device_id_type=MESH)

    def own(l, i):
        src, dst = ((g_in, first(KI)), (g_out, pl.ds(KI, NO)))[i]
        return local(src.at[base + l], gbuf.at[l, dst], gl_sem.at[l, i])

    def swap(l, i):
        src, dst = ((g_in, first(KI)), (g_out, pl.ds(KI, NO)))[i]
        return remote(src.at[pbase + l], pbuf.at[l, dst], gs_sem.at[l, i], gr_sem.at[l, i], partner)

    my_rows, its_rows = pl.ds(base, LC), pl.ds(pbase, LC)
    loads = [local(m_in, mraw_in, ml_sem.at[0]), local(m_out, mraw_out, ml_sem.at[1]),
             local(r_in.at[my_rows], lraw.at[0, c], ol_sem.at[0]), local(c_out.at[my_rows], lraw.at[1, c], ol_sem.at[1]),
             local(c_in.at[my_rows], craw, ol_sem.at[2]), local(r_out.at[my_rows], oraw, ol_sem.at[3])]
    w_loads = [local(w_in, wn_in, wl_sem.at[0]), local(w_out, wn_out, wl_sem.at[1])]

    def lane_swap(m, core):
        return remote((r_in, c_out)[m].at[its_rows], lraw.at[m, core], os_sem.at[m], or_sem.at[m], partner)

    def start_loads(l, carry):
        own(l, 0).start()
        own(l, 1).start()
        return carry

    lax.fori_loop(0, LC, start_loads, 0)
    for copy in loads:
        copy.start()
    pl.semaphore_wait(barrier, len(peers))
    for l in range(OB):
        swap(l, 0).start()
        swap(l, 1).start()
    lane_swap(0, c).start()
    lane_swap(1, c).start()
    rvacc[...] = jnp.zeros_like(rvacc)
    lvacc[...] = jnp.zeros_like(lvacc)

    lane, lane8, row8, row16 = lane_of((Q, LN)), lane_of((8, LN)), row_of((8, LN)), row_of((16, LN))
    m96, k96 = lane < B96, lane8 < B96
    head = row_of((Q, LN)) < HEAD
    only_x, only_yz = row16 >= 12, (row16 >= 8) & (row16 < 12)

    def way(l):
        return 1 - 2 * (l % 2)

    def ahead(l):
        return (x + way(l) + RING) % RING

    def behind(l):
        return (x - way(l) + RING) % RING

    across = (x + 2) % RING

    def step1(l):
        return remote(pack.at[l, across], via.at[l], s_sem.at[l, 0], via_sem.at[l], at_x(ahead(l)))

    def step2(l):
        return remote(pack.at[l, ahead(l)], rin.at[l, 0], s_sem.at[l, 1], rin_sem.at[l, 0], at_x(ahead(l)))

    def step3(l):
        return remote(pack.at[l, behind(l)], rin.at[l, 1], s_sem.at[l, 2], rin_sem.at[l, 1], at_x(behind(l)))

    def m_rows(core):
        return pl.ds(pl.multiple_of(core * B48, 16), B48)

    def moment_swap(l, core):
        return remote(msend.at[l], mt.at[l, m_rows(core)], ms_sem.at[l], mr_sem.at[l], partner)

    def stage_a(l):
        for i in range(2):
            own(l, i).wait()
            swap(l, i).wait_recv()

        def tile(t, q):
            return gbuf[l, block(q), tile_cols(t)] + pbuf[l, block(q), tile_cols(t)]

        def chunk(d, q):
            if d == 0:
                return tile(0, q)
            if d == 1:
                return roll(jnp.where(m96, tile(1, q), tile(0, q)), 32)
            if d == 2:
                return roll(jnp.where(lane < 64, tile(2, q), tile(1, q)), 64)
            return roll(tile(2, q), B96)

        for d in range(RING):
            for i, val in enumerate(join_quarters([chunk(d, q) for q in range(4)], m96)):
                pack[l, d, block(i), :] = val
        step1(l).start()
        step3(l).start()

    def stage_n(l):
        msend[l, :, first(KI)] = mraw_in[pbase + l].astype(F32)
        msend[l, :, pl.ds(MID, NO)] = mraw_out[pbase + l].astype(F32)
        moment_swap(l, c).start()
        mt[l, m_rows(c), first(KI)] = mraw_in[base + l].astype(F32)
        mt[l, m_rows(c), pl.ds(MID, NO)] = mraw_out[base + l].astype(F32)

    def stage_b(l):
        step1(l).wait_recv()
        to = ahead(l)
        pack[l, to] = pack[l, to] + via[l]
        step2(l).start()

    def stage_c(l):
        step2(l).wait_recv()
        step3(l).wait_recv()
        sq = []
        for i in range(3):
            grad = pack[l, x, block(i), :] + rin[l, 0, block(i), :] + rin[l, 1, block(i), :]
            fin[l, block(i), :] = grad
            sq.append(grad * grad + 1e-30)
        g, lg = l // LG, l % LG
        sums = [rowsum(pick(m96, val)) for val in sq]
        sums.append(rowsum(jnp.where(m96, 0.0, sq[0] + sq[1] + sq[2])))
        acc = rvacc[g, first(Q), :]
        for q in range(4):
            acc = jnp.where(lane == LG * q + lg, sums[q], acc)
        rvacc[g, first(Q), :] = acc
        top = colsum(pick(head, sq[2]))
        low = colsum(jnp.where(head, 0.0, sq[2]))
        cols = [colsum(sq[0]), colsum(sq[1])]
        wide = [jnp.broadcast_to(val, (8, LN)) for val in (cols[0], cols[1], top + low)]
        in_sum = pick(k96, cols[0] + cols[1] + top)
        out_sum = pick(k96, low + last_quarter(wide))
        both = jnp.where(row8 == lg, in_sum, lvacc[g])
        lvacc[g] = jnp.where(row8 == LG + lg, out_sum, both)

    def stage_m(l):
        moment_swap(l, other).wait_recv()
        val = mt[l].T
        third = jnp.concatenate([val[2 * Q:KI], val[MID:MID + B48]], axis=0)
        quarters = [val[:Q], val[Q:2 * Q], third, val[MID + B48:MID + NO]]
        for i, part in enumerate(join_quarters(quarters, m96)):
            mpack[l, block(i), :] = part

    boxes = {RV: (box_rv, x, at_x), LY: (box_ly, y, at_y), LZ: (box_lz, z, at_z),
             SX: (box_sx, x, at_x), SY: (box_sy, y, at_y), SZ: (box_sz, z, at_z)}

    def box_copy(kind, g, k, slot):
        box, me, place = boxes[kind]
        return remote(box.at[g, slot], box.at[g, slot], sts_sem.at[g, kind, k - 1], str_sem.at[g, kind, slot], place(me + k))

    def post(kind, g, val):
        box, me, place = boxes[kind]
        box[g, me] = val
        for k in range(1, RING):
            box_copy(kind, g, k, me).start()

    def collect(kind, g):
        box, me, place = boxes[kind]
        for k in range(1, RING):
            box_copy(kind, g, k, (me + k) % RING).wait_recv()
        return ((box[g, 0] + box[g, 1]) + box[g, 2]) + box[g, 3]

    def sums_send(g):
        post(LY, g, lvacc[g])
        post(RV, g, rvacc[g].T[:16])

    def sums_mid(g):
        post(LZ, g, collect(LY, g))

    beta = beta_ref[0]

    def old_vectors():
        for copy in loads[2:]:
            copy.wait()
        for m in range(2):
            lane_swap(m, other).wait_recv()
            for core in range(2):
                pads[m, core, :, first(B48)] = lraw[m, core]
        pads[2, 0, :, first(KI - LN)] = craw[:, pl.ds(LN, KI - LN)]
        pads[2, 1, :, first(NO)] = oraw[...]
        low, high, rest = craw[:, first(LN)], pads[2, 0], pads[2, 1]
        lanes = [jnp.where(lane8 < B48, pads[m, 0], roll(pads[m, 1], B48)) for m in range(2)]
        rows = [low, jnp.where(lane8 < LN - Q, roll(low, -Q), roll(high, -Q)),
                jnp.where(lane8 < HEAD, roll(high, -16), roll(rest, HEAD)), roll(rest, -B48)]
        for g in range(NG):
            part = slice(LG * g, LG * g + LG)
            lvold[g] = jnp.concatenate([val[part] for val in lanes], axis=0)
            rvold[g] = jnp.concatenate([val[part] for val in rows], axis=0)

    def vec_swap(g, half, i):
        ref = (lvnew, rvnew)[i]
        return remote(ref.at[half, g], ref.at[half, g], vs_sem.at[g, i], vr_sem.at[g, i], partner)

    def moments(g):
        lv_mean = collect(LZ, g) / jnp.where(row8 < LG, KIN, NOUT)
        lv_new = beta * lvold[g] + (1.0 - beta) * lv_mean
        lvnew[c, g] = lv_new
        rv_new = beta * rvold[g] + (1.0 - beta) * (collect(RV, g) / NI)
        rvnew[c, g] = rv_new
        for i in range(2):
            vec_swap(g, c, i).start()
        scale_l = 1.0 / jnp.sqrt(jnp.where(k96, lv_new, 1.0))
        scale_r = 1.0 / jnp.sqrt(jnp.where(lane_of((16, LN)) < Q, rv_new, 1.0))
        wide = jnp.concatenate([scale_r, jnp.ones((LN - 16, LN), F32)], axis=0).T
        tots = jnp.zeros((16, LN), F32)
        lane1 = lane_of((1, LN))
        for lg in range(LG):
            l = g * LG + lg
            rs = [jnp.broadcast_to(wide[:Q, LG * q + lg:LG * q + lg + 1], (Q, LN)) for q in range(4)]
            sc_in = scale_l[lg:lg + 1, :]
            sc_out = jnp.broadcast_to(scale_l[LG + lg:LG + lg + 1, :], (8, LN))
            parts = []
            for i in range(3):
                body = jnp.where(head, sc_in, sc_out[:1]) if i == 2 else sc_in
                lanes = jnp.where(m96, body, roll(sc_out, B96 - 32 * i)[:1])
                u0 = fin[l, block(i), :] * jnp.where(m96, rs[i], rs[3]) * lanes
                fin[l, block(i), :] = u0
                parts.append(u0 * u0)
            inner = pick(m96, parts[0] + parts[1] + pick(head, parts[2]))
            outer = jnp.where(m96, jnp.where(head, 0.0, parts[2]), parts[0] + parts[1] + parts[2])
            v_in = pick(lane1 < B96, lv_new[lg:lg + 1, :])
            v_out = pick((lane1 >= HEAD) & (lane1 < Q), rv_new[8 + lg:9 + lg, :]) + pick(lane1 < Q, rv_new[12 + lg:13 + lg, :])
            for k, val in enumerate((colsum(inner), colsum(outer), v_in, v_out)):
                tots = jnp.where(row16 == LG * k + lg, val, tots)
        post(SY, g, tots)

    def totals_y(g):
        post(SZ, g, jnp.where(only_yz, box_sy[g, y], collect(SY, g)))

    def totals_z(g):
        post(SX, g, jnp.where(only_yz, box_sz[g, z], collect(SZ, g)))

    def factors(g):
        tot = rowsum(jnp.where(only_x, box_sx[g, x], collect(SX, g)))
        isin = row_of((8, 1)) < LG
        mean_r = tot[8:] / jnp.where(isin, NI, NOUT)
        rms = jnp.sqrt(mean_r * tot[:8] / jnp.where(isin, NI * KIN, NOUT * KO))
        return jnp.sqrt(mean_r) / jnp.maximum(1.0, rms)

    def update(l, lg, fac):
        f_in, f_out = fac[lg:lg + 1, :], fac[LG + lg:LG + lg + 1, :]
        for i in range(3):
            upd = fin[l, block(i), :] * jnp.where((m96 & head) if i == 2 else m96, f_in, f_out)
            new = 0.9 * mpack[l, block(i), :] + 0.1 * upd
            mall[base + l, x, block(i), :] = new.astype(BF16).astype(F32)

    def gather(l, k):
        slot = x if k < 2 else behind(l)
        ref = mall.at[base + l, slot]
        return remote(ref, ref, ags_sem.at[l, k], agr_sem.at[l, k], at_x(behind(l) if k == 1 else ahead(l)))

    def arrival(l, k):
        ref = mall.at[base + l, (behind(l), ahead(l), across)[k]]
        return remote(ref, ref, ags_sem.at[l, k], agr_sem.at[l, k], at_x(ahead(l)))

    def share(l, k, start):
        ref = mall.at[start + l, (behind(l), ahead(l), across, x)[k]]
        return remote(ref, ref, shs_sem.at[l, k], shr_sem.at[l, k], partner)

    def send_pair(l):
        gather(l, 0).start()
        gather(l + 1, 0).start()
        gather(l, 1).start()
        gather(l + 1, 1).start()
        share(l, 3, base).start()
        share(l + 1, 3, base).start()

    def forward_pair(l):
        for k in (l, l + 1):
            arrival(k, 0).wait_recv()
            gather(k, 2).start()
            share(k, 0, base).start()

    def settle_pair(l):
        for k in (l, l + 1):
            for i in (1, 2):
                arrival(k, i).wait_recv()
                share(k, i, base).start()

    rate = rate_ref[0]
    decay = rate * wd_ref[0]

    def unpack(at):
        for q in range(4):
            if q < 3:
                chunk = [mall[at, d, block(q), :] for d in range(RING)]
            else:
                chunk = [last_quarter([mall[at, d, block(i), :] for i in range(3)]) for d in range(RING)]
            r1, r2, r3 = roll(chunk[1], B96), roll(chunk[2], 64), roll(chunk[3], 32)
            mom = (jnp.where(m96, chunk[0], r1), jnp.where(lane < 64, r1, r2), jnp.where(lane < 32, r2, r3))
            spots = (((wn_in, 0, 0, Q),), ((wn_in, Q, 0, Q),), ((wn_in, 2 * Q, 0, HEAD), (wn_out, 0, HEAD, B48)), ((wn_out, B48, 0, Q),))[q]
            for t in range(3):
                for ref, dst, src, num in spots:
                    rows = pl.ds(dst, num)
                    w = ref[at, rows, tile_cols(t)]
                    ref[at, rows, tile_cols(t)] = w - rate * mom[t][src:src + num] - decay * w
        parts = [mall[at, x, block(i), :] for i in range(3)]
        parts.append(last_quarter(parts))
        spots = ((0, 0, Q),), ((Q, 0, Q),), ((2 * Q, 0, HEAD), (MID, HEAD, B48)), ((MID + B48, 0, Q),)
        for val, places in zip(parts, spots):
            val = jnp.where(c == 0, val, roll(val, -B48))
            for dst, src, num in places:
                tall[pl.ds(dst, num), :] = val[src:src + num]
        turned = [tall[tile_cols(t), :].T[:B48] for t in range(3)]
        mn_in[at, :, first(LN)] = turned[0].astype(BF16)
        mn_in[at, :, pl.ds(LN, KI - LN)] = turned[1][:, :KI - LN].astype(BF16)
        mn_out[at] = turned[2][:, :NO].astype(BF16)

    def unpack_pair(l, start):
        lax.fori_loop(start + l, start + l + 2, lambda at, carry: (unpack(at), carry)[1], 0)

    def take_pair(l):
        for k in (l, l + 1):
            for i in range(4):
                share(k, i, pbase).wait_recv()
        unpack_pair(l, pbase)

    def new_vectors():
        lane4 = lane_of((LG, LN))
        for half in range(2):
            for g in range(NG):
                rows = pl.ds(LC * half + LG * g, LG)
                both, val = lvnew[half, g], rvnew[half, g]
                both = jnp.where(c == 0, both, roll(both, -B48))
                rn_in[rows, :] = both[:LG, :B48]
                cn_out[rows, :] = both[LG:, :B48]
                two, three = roll(val, Q)[LG:8], val[8:12]
                cn_in[rows, first(LN)] = jnp.where(lane4 < Q, val[:LG], two)
                cn_in[rows, pl.ds(LN, KI - LN)] = jnp.where(lane4 < 16, two, roll(val, 16)[8:12])[:, :KI - LN]
                rn_out[rows, :] = jnp.where(lane4 < B48, roll(val, -HEAD)[8:12], roll(val, B48)[12:])[:, :NO]

    def stage(it, carry):
        @pl.when(it < LC)
        def _():
            stage_a(it)

        @pl.when(it < LC - OB)
        def _():
            swap(it + OB, 0).start()
            swap(it + OB, 1).start()

        @pl.when(it == 0)
        def _():
            loads[0].wait()
            loads[1].wait()

        @pl.when((it >= OB) & (it < LC + OB))
        def _():
            stage_b(it - OB)

        @pl.when(it < LC)
        def _():
            stage_n(it)

        @pl.when(it >= OC)
        def _():
            stage_c(it - OC)
            stage_m(it - OC)

        @pl.when(it == OC)
        def _():
            w_loads[0].start()
            w_loads[1].start()
            old_vectors()

        @pl.when(it == OC + 3)
        def _():
            sums_send(0)

        @pl.when(it == OC + 4)
        def _():
            sums_mid(0)

        @pl.when(it == OC + 5)
        def _():
            moments(0)

        @pl.when(it == OC + 6)
        def _():
            totals_y(0)

        @pl.when(it == OC + 7)
        def _():
            totals_z(0)

        return carry

    lax.fori_loop(0, LC + OC, stage, 0)
    sums_send(1)
    fac = factors(0)
    for lg in range(LG):
        update(lg, lg, fac)
        if lg == 1:
            send_pair(0)
    sums_mid(1)
    forward_pair(0)
    send_pair(2)
    moments(1)
    totals_y(1)
    forward_pair(2)
    totals_z(1)
    settle_pair(0)
    settle_pair(2)
    w_loads[0].wait()
    w_loads[1].wait()
    unpack_pair(0, base)
    fac = factors(1)
    for lg in range(LG):
        update(LG + lg, lg, fac)
        if lg == 1:
            send_pair(4)
    unpack_pair(2, base)
    take_pair(0)
    forward_pair(4)
    send_pair(6)
    take_pair(2)
    for g in range(NG):
        for i in range(2):
            vec_swap(g, other, i).wait_recv()
    new_vectors()
    settle_pair(4)
    unpack_pair(4, base)
    forward_pair(6)
    take_pair(4)
    settle_pair(6)
    unpack_pair(6, base)
    take_pair(6)

    def drain(l, carry):
        for i in range(2):
            swap(l, i).wait_send()
        moment_swap(l, c).wait_send()
        for step in (step1, step2, step3):
            step(l).wait_send()
        for k in range(3):
            gather(l, k).wait_send()
        for k in range(4):
            share(l, k, base).wait_send()
        return carry

    lax.fori_loop(0, LC, drain, 0)
    for m in range(2):
        lane_swap(m, c).wait_send()
    for g in range(NG):
        for kind in KINDS:
            for k in range(1, RING):
                box_copy(kind, g, k, boxes[kind][1]).wait_send()
        for i in range(2):
            vec_swap(g, c, i).wait_send()


def update_call(scalars, arrays):
    hbm, smem = pl.BlockSpec(memory_space=pltpu.HBM), pl.BlockSpec(memory_space=pltpu.SMEM)
    dma, vmem = pltpu.SemaphoreType.DMA, pltpu.VMEM

    def lanes(*lead):
        return vmem(lead + (LN,), F32)

    scratch = [
        vmem((LC, KI + NO, D), F32), vmem((LC, KI + NO, D), F32), lanes(LC, RING, CH), lanes(LC, CH), lanes(LC, 2, CH), lanes(LC, CH),
        lanes(L, RING, CH), vmem((L, B48, KI), BF16), vmem((L, B48, NO), BF16), vmem((LC, B48, D), F32), vmem((LC, LN, D), F32),
        lanes(LC, CH), lanes(D), lanes(NG, LN), lanes(NG, 8),
        vmem((2, 2, LC, B48), F32), vmem((LC, KI), F32), vmem((LC, NO), F32), lanes(3, 2, LC),
        lanes(NG, 8), lanes(NG, 16), lanes(2, NG, 8), lanes(2, NG, 16),
        lanes(NG, RING, 16), lanes(NG, RING, 8), lanes(NG, RING, 8), lanes(NG, RING, 16), lanes(NG, RING, 16), lanes(NG, RING, 16),
        dma((LC, 2)), dma((LC, 2)), dma((LC, 2)), dma((2,)), dma((LC,)), dma((LC,)), dma((LC, 3)), dma((LC,)), dma((LC, 2)),
        dma((LC, 3)), dma((LC, 3)), dma((LC, 4)), dma((LC, 4)), dma((NG, len(KINDS), 3)), dma((NG, len(KINDS), RING)),
        dma((NG, 2)), dma((NG, 2)), dma((4,)), dma((2,)), dma((2,)), dma((2,)),
    ]
    outs = [((L, KI, D), F32), ((L, NO, D), F32), ((L, B48, KI), BF16), ((L, B48, NO), BF16),
            ((L, B48), F32), ((L, KI), F32), ((L, NO), F32), ((L, B48), F32)]
    return pl.pallas_call(
        kernel,
        out_shape=[vmem(*out) for out in outs],
        in_specs=[smem] * len(scalars) + [hbm] * len(arrays),
        out_specs=[pl.BlockSpec(memory_space=vmem)] * len(outs),
        scratch_shapes=scratch,
        compiler_params=pltpu.CompilerParams(collective_id=0, has_side_effects=True, vmem_limit_bytes=36 * 2**20),
        name='adafactor',
    )(*[val.reshape(1) for val in scalars], *[pltpu.with_memory_space_constraint(val, pltpu.HBM) for val in arrays])


def solution(mesh):
    def turn(val):
        return val.swapaxes(1, 2)

    def body(w_in, w_out, g_in, g_out, m_in, m_out, r_in, c_in, r_out, c_out, learn_rate, weight_decay, beta_two):
        out = update_call((learn_rate, weight_decay, beta_two),
                          (turn(w_in), w_out, turn(g_in[0]), g_out[0], m_in, turn(m_out), r_in, c_in, r_out, c_out))
        return (turn(out[0]), out[1], out[2], turn(out[3])) + tuple(out[4:])

    cols, rows, own = P(None, None, 'tp'), P(None, 'tp', None), P(None, 'dp')
    outs = (cols, rows, P(None, 'dp', 'tp'), P(None, 'tp', 'dp'), own, P(None, 'tp'), P(None, 'tp'), own)
    in_specs = (cols, rows, P('dp', *cols), P('dp', *rows)) + outs[2:] + (P(), P(), P())
    return jax.shard_map(body, mesh=mesh, in_specs=in_specs, out_specs=outs, check_vma=False)
```

time: 350 us -> 99.6 us (0.28)
  blocking collectives: 177 us -> 0 us
  waiting for transfers between devices: 107 us -> 0 us
  Pallas kernels: 0 us -> 89.4 us
  local copies, waits for them, and re-layouts: 28.1 us -> 7.41 us
  other arithmetic: 20.4 us -> 0 us
  between operations: 15.8 us -> 2.59 us
    psum x4 -> x0, blocking collectives: 177 us -> none  [the longest x2 76.2 us: local_update(): row_mean = lax.psum(jnp.sum(grad_sq, axis=2), col_axis) / n_cols]
    pallas_call x0 -> x1, Pallas kernels: none -> 89.4 us  [update_call(): pl.pallas_call(kernel, out_shape=[vmem(*out) for out in outs], in_specs=[...]
    all_gather x2 -> x0, waiting for transfers between devices: 54.7 us -> none  [local_update(): w_new = lax.all_gather(w_block, 'dp', axis=dp_dim, tiled=True)]
    reduce_scatter x2 -> x0, waiting for transfers between devices: 52.4 us -> none  [local_update(): lax.psum_scatter(grad_rep[0], 'dp', scatter_dimension=dp_dim, tiled=True)]
    unnamed x26 -> x8, local copies, waits for them, and re-layouts: 23.5 us -> 7.41 us
    reduce_sum x6 -> x0, other arithmetic: 11.5 us -> none  [the longest x2 3.91 us: local_update(): total_sq = lax.psum(jnp.sum(update * update, axis=(1, 2)), ('tp', 'dp'))]
    sub x2 -> x0, other arithmetic: 4.92 us -> none  [local_update(): w_block - learn_rate * mom_new.astype(jnp.float32)]
    dynamic_slice x2 -> x0, local copies, waits for them, and re-layouts: 4.61 us -> none  [local_update(): lax.dynamic_slice_in_dim(weight, lax.axis_index('dp') * width, width, axi...]
  transfers between devices with their start and end apart: 4 -> 0, of which waited for: 4 -> 0; matrix products, arithmetic and copies ran while one was open for 7% -> 0% of each run, Pallas kernels for 0% -> 0%
where the time goes in v1:
time: 99.6 us; the launch traced here: 99.4 us
  Pallas kernels  89.4 us (90%)
  local copies, waits for them, and re-layouts  7.41 us (7%)
  between operations  2.59 us (3%)
    pallas_call x1, Pallas kernels, update_call(): pl.pallas_call(kernel, out_shape=[vmem(*out) for out in outs], in_specs=[...  89.4 us
    unnamed x8, local copies, waits for them, and re-layouts  7.41 us

profile of v1, /device:TPU:1, one launch (start us, length us, event | category | flops | bytes accessed | tf_op | source)
XLA Modules:
  0.0 99.4 jit_solution(2368959564909301350)
XLA Ops:
  2.6 89.4 %adafactor.1 = (f32[16,168,384]{2,1,0:T(8,128)S(1)}, f32[16,120,384]{2,1,0:T(8,128)S(1)}, bf16[16,48,168]{2,1,0:T(8,128)(2,1)S(1)}, bf16[16,48,120]{2,1,0:T(8,12...) custom-call(f32[1]{0:T(128)} %bitcast.11.rate_ref, ...), custom_call_target="tpu_custom_call" | custom-call | tf_op jit(solution)/shard_map/adafactor/pallas_call | solution.py:564
  92.0 2.0 %copy.29 = f32[16,384,168]{1,2,0:T(8,128)} copy(f32[16,384,168]{1,2,0:T(8,128)S(1)} %bitcast.14) | data formatting | bytes 8257536
  94.0 0.6 copy.33
  94.6 0.6 copy.35
  95.2 0.6 copy.36
  95.8 0.6 copy.34
  96.4 0.7 copy.32
  97.1 0.7 copy.31
  97.8 1.6 %copy.30 = f32[16,120,384]{2,1,0:T(8,128)} copy(f32[16,120,384]{2,1,0:T(8,128)S(1)} %get-tuple-element.25) | data formatting | bytes 5898240

commit v2 on v1

--- a/solution.py
+++ b/solution.py
@@ -10,12 +10,12 @@
 RING = 4
 L, D = 16, 384
 KI, NO = 168, 120
-LC, LG, NG = 8, 4, 2
+LC, LG, NG = 8, 2, 4
 Q, LN, B48, B96 = 72, 128, 48, 96
 CH, HEAD, MID = 3 * Q, KI - 2 * Q, 256
 NI, KIN, NOUT, KO = 384.0, 2688.0, 1920.0, 384.0
 KINDS = RV, LY, LZ, SY, SZ, SX = range(6)
-OB, OC = 2, 4
+AHEAD = 2
 
 
 def roll(val, shift):
@@ -126,7 +126,7 @@
     for copy in loads:
         copy.start()
     pl.semaphore_wait(barrier, len(peers))
-    for l in range(OB):
+    for l in range(AHEAD * LG):
         swap(l, 0).start()
         swap(l, 1).start()
     lane_swap(0, c).start()
@@ -134,10 +134,10 @@
     rvacc[...] = jnp.zeros_like(rvacc)
     lvacc[...] = jnp.zeros_like(lvacc)
 
-    lane, lane8, row8, row16 = lane_of((Q, LN)), lane_of((8, LN)), row_of((8, LN)), row_of((16, LN))
+    lane, lane8, row8 = lane_of((Q, LN)), lane_of((8, LN)), row_of((8, LN))
     m96, k96 = lane < B96, lane8 < B96
     head = row_of((Q, LN)) < HEAD
-    only_x, only_yz = row16 >= 12, (row16 >= 8) & (row16 < 12)
+    no_x, only_x = row8 >= 3 * LG, (row8 >= 2 * LG) & (row8 < 3 * LG)
 
     def way(l):
         return 1 - 2 * (l % 2)
@@ -254,7 +254,7 @@
 
     def sums_send(g):
         post(LY, g, lvacc[g])
-        post(RV, g, rvacc[g].T[:16])
+        post(RV, g, rvacc[g].T[:8])
 
     def sums_mid(g):
         post(LZ, g, collect(LY, g))
@@ -276,7 +276,7 @@
                 jnp.where(lane8 < HEAD, roll(high, -16), roll(rest, HEAD)), roll(rest, -B48)]
         for g in range(NG):
             part = slice(LG * g, LG * g + LG)
-            lvold[g] = jnp.concatenate([val[part] for val in lanes], axis=0)
+            lvold[g] = jnp.concatenate([val[part] for val in lanes + lanes], axis=0)
             rvold[g] = jnp.concatenate([val[part] for val in rows], axis=0)
 
     def vec_swap(g, half, i):
@@ -292,9 +292,9 @@
         for i in range(2):
             vec_swap(g, c, i).start()
         scale_l = 1.0 / jnp.sqrt(jnp.where(k96, lv_new, 1.0))
-        scale_r = 1.0 / jnp.sqrt(jnp.where(lane_of((16, LN)) < Q, rv_new, 1.0))
-        wide = jnp.concatenate([scale_r, jnp.ones((LN - 16, LN), F32)], axis=0).T
-        tots = jnp.zeros((16, LN), F32)
+        scale_r = 1.0 / jnp.sqrt(jnp.where(lane8 < Q, rv_new, 1.0))
+        wide = jnp.concatenate([scale_r, jnp.ones((LN - 8, LN), F32)], axis=0).T
+        tots = jnp.zeros((8, LN), F32)
         lane1 = lane_of((1, LN))
         for lg in range(LG):
             l = g * LG + lg
@@ -311,22 +311,22 @@
             inner = pick(m96, parts[0] + parts[1] + pick(head, parts[2]))
             outer = jnp.where(m96, jnp.where(head, 0.0, parts[2]), parts[0] + parts[1] + parts[2])
             v_in = pick(lane1 < B96, lv_new[lg:lg + 1, :])
-            v_out = pick((lane1 >= HEAD) & (lane1 < Q), rv_new[8 + lg:9 + lg, :]) + pick(lane1 < Q, rv_new[12 + lg:13 + lg, :])
+            v_out = pick((lane1 >= HEAD) & (lane1 < Q), rv_new[2 * LG + lg:2 * LG + lg + 1, :]) + pick(lane1 < Q, rv_new[3 * LG + lg:3 * LG + lg + 1, :])
             for k, val in enumerate((colsum(inner), colsum(outer), v_in, v_out)):
-                tots = jnp.where(row16 == LG * k + lg, val, tots)
+                tots = jnp.where(row8 == LG * k + lg, val, tots)
         post(SY, g, tots)
 
     def totals_y(g):
-        post(SZ, g, jnp.where(only_yz, box_sy[g, y], collect(SY, g)))
+        post(SZ, g, jnp.where(only_x, box_sy[g, y], collect(SY, g)))
 
     def totals_z(g):
-        post(SX, g, jnp.where(only_yz, box_sz[g, z], collect(SZ, g)))
+        post(SX, g, jnp.where(only_x, box_sz[g, z], collect(SZ, g)))
 
     def factors(g):
-        tot = rowsum(jnp.where(only_x, box_sx[g, x], collect(SX, g)))
-        isin = row_of((8, 1)) < LG
-        mean_r = tot[8:] / jnp.where(isin, NI, NOUT)
-        rms = jnp.sqrt(mean_r * tot[:8] / jnp.where(isin, NI * KIN, NOUT * KO))
+        tot = rowsum(jnp.where(no_x, box_sx[g, x], collect(SX, g)))
+        isin = row_of((2 * LG, 1)) < LG
+        mean_r = tot[2 * LG:] / jnp.where(isin, NI, NOUT)
+        rms = jnp.sqrt(mean_r * tot[:2 * LG] / jnp.where(isin, NI * KIN, NOUT * KO))
         return jnp.sqrt(mean_r) / jnp.maximum(1.0, rms)
 
     def update(l, lg, fac):
@@ -415,96 +415,107 @@
                 both, val = lvnew[half, g], rvnew[half, g]
                 both = jnp.where(c == 0, both, roll(both, -B48))
                 rn_in[rows, :] = both[:LG, :B48]
-                cn_out[rows, :] = both[LG:, :B48]
-                two, three = roll(val, Q)[LG:8], val[8:12]
+                cn_out[rows, :] = both[LG:2 * LG, :B48]
+                two = roll(val, Q)[LG:2 * LG]
                 cn_in[rows, first(LN)] = jnp.where(lane4 < Q, val[:LG], two)
-                cn_in[rows, pl.ds(LN, KI - LN)] = jnp.where(lane4 < 16, two, roll(val, 16)[8:12])[:, :KI - LN]
-                rn_out[rows, :] = jnp.where(lane4 < B48, roll(val, -HEAD)[8:12], roll(val, B48)[12:])[:, :NO]
+                cn_in[rows, pl.ds(LN, KI - LN)] = jnp.where(lane4 < 16, two, roll(val, 16)[2 * LG:3 * LG])[:, :KI - LN]
+                rn_out[rows, :] = jnp.where(lane4 < B48, roll(val, -HEAD)[2 * LG:3 * LG], roll(val, B48)[3 * LG:])[:, :NO]
+
+    def both(step, g):
+        for lg in range(LG):
+            step(LG * g + lg)
+
+    def swap_start(l):
+        swap(l, 0).start()
+        swap(l, 1).start()
 
     def stage(it, carry):
-        @pl.when(it < LC)
-        def _():
-            stage_a(it)
-
-        @pl.when(it < LC - OB)
-        def _():
-            swap(it + OB, 0).start()
-            swap(it + OB, 1).start()
+        @pl.when(it < NG)
+        def _():
+            both(stage_a, it)
+
+        @pl.when(it < NG - AHEAD)
+        def _():
+            both(swap_start, it + AHEAD)
 
         @pl.when(it == 0)
         def _():
             loads[0].wait()
             loads[1].wait()
 
-        @pl.when((it >= OB) & (it < LC + OB))
-        def _():
-            stage_b(it - OB)
-
-        @pl.when(it < LC)
-        def _():
-            stage_n(it)
-
-        @pl.when(it >= OC)
-        def _():
-            stage_c(it - OC)
-            stage_m(it - OC)
-
-        @pl.when(it == OC)
+        @pl.when((it >= 1) & (it <= NG))
+        def _():
+            both(stage_b, it - 1)
+
+        @pl.when(it == 4)
+        def _():
+            totals_y(0)
+
+        @pl.when((it == 3) | (it == 4))
+        def _():
+            sums_mid(it - 3)
+
+        @pl.when(it < NG)
+        def _():
+            both(stage_n, it)
+
+        @pl.when(it == 2)
         def _():
             w_loads[0].start()
             w_loads[1].start()
             old_vectors()
 
-        @pl.when(it == OC + 3)
-        def _():
-            sums_send(0)
-
-        @pl.when(it == OC + 4)
-        def _():
-            sums_mid(0)
-
-        @pl.when(it == OC + 5)
-        def _():
-            moments(0)
-
-        @pl.when(it == OC + 6)
-        def _():
-            totals_y(0)
-
-        @pl.when(it == OC + 7)
+        @pl.when(it >= 2)
+        def _():
+            both(stage_c, it - 2)
+            sums_send(it - 2)
+            both(stage_m, it - 2)
+
+        @pl.when(it == 4)
         def _():
             totals_z(0)
 
+        @pl.when((it == 3) | (it == 4))
+        def _():
+            moments(it - 3)
+
         return carry
 
-    lax.fori_loop(0, LC + OC, stage, 0)
-    sums_send(1)
-    fac = factors(0)
-    for lg in range(LG):
-        update(lg, lg, fac)
-        if lg == 1:
-            send_pair(0)
-    sums_mid(1)
+    lax.fori_loop(0, NG + 2, stage, 0)
+
+    def update_pair(g):
+        fac = factors(g)
+        for lg in range(LG):
+            update(LG * g + lg, lg, fac)
+
+    update_pair(0)
+    send_pair(0)
+    totals_y(1)
+    sums_mid(2)
+    totals_z(1)
+    moments(2)
+    sums_mid(3)
     forward_pair(0)
+    update_pair(1)
     send_pair(2)
-    moments(1)
-    totals_y(1)
+    totals_y(2)
+    moments(3)
+    totals_z(2)
+    totals_y(3)
+    settle_pair(0)
     forward_pair(2)
-    totals_z(1)
-    settle_pair(0)
-    settle_pair(2)
     w_loads[0].wait()
     w_loads[1].wait()
     unpack_pair(0, base)
-    fac = factors(1)
-    for lg in range(LG):
-        update(LG + lg, lg, fac)
-        if lg == 1:
-            send_pair(4)
-    unpack_pair(2, base)
+    totals_z(3)
+    update_pair(2)
+    send_pair(4)
     take_pair(0)
+    settle_pair(2)
+    update_pair(3)
     forward_pair(4)
     send_pair(6)
+    unpack_pair(2, base)
     take_pair(2)
     for g in range(NG):
         for i in range(2):
@@ -553,8 +564,8 @@
         lanes(L, RING, CH), vmem((L, B48, KI), BF16), vmem((L, B48, NO), BF16), vmem((LC, B48, D), F32), vmem((LC, LN, D), F32),
         lanes(LC, CH), lanes(D), lanes(NG, LN), lanes(NG, 8),
         vmem((2, 2, LC, B48), F32), vmem((LC, KI), F32), vmem((LC, NO), F32), lanes(3, 2, LC),
-        lanes(NG, 8), lanes(NG, 16), lanes(2, NG, 8), lanes(2, NG, 16),
-        lanes(NG, RING, 16), lanes(NG, RING, 8), lanes(NG, RING, 8), lanes(NG, RING, 16), lanes(NG, RING, 16), lanes(NG, RING, 16),
+        lanes(NG, 8), lanes(NG, 8), lanes(2, NG, 8), lanes(2, NG, 8),
+        *[lanes(NG, RING, 8)] * len(KINDS),
         dma((LC, 2)), dma((LC, 2)), dma((LC, 2)), dma((2,)), dma((LC,)), dma((LC,)), dma((LC, 3)), dma((LC,)), dma((LC, 2)),
         dma((LC, 3)), dma((LC, 3)), dma((LC, 4)), dma((LC, 4)), dma((NG, len(KINDS), 3)), dma((NG, len(KINDS), RING)),
         dma((NG, 2)), dma((NG, 2)), dma((4,)), dma((2,)), dma((2,)), dma((2,)),
@@ -572,13 +583,35 @@
     )(*[val.reshape(1) for val in scalars], *[pltpu.with_memory_space_constraint(val, pltpu.HBM) for val in arrays])
 
 
+def store_kernel(*refs):
+    num = len(refs) // 2
+    copies = [pltpu.make_async_copy(src, dst, refs[-1].at[i]) for i, (src, dst) in enumerate(zip(refs[:num], refs[num:-1]))]
+    for copy in copies:
+        copy.start()
+    for copy in copies:
+        copy.wait()
+
+
+def store_call(vals):
+    anyspace = pl.BlockSpec(memory_space=pl.ANY)
+    return pl.pallas_call(
+        store_kernel,
+        out_shape=[jax.ShapeDtypeStruct(val.shape, val.dtype) for val in vals],
+        in_specs=[anyspace] * len(vals),
+        out_specs=[anyspace] * len(vals),
+        scratch_shapes=[pltpu.SemaphoreType.DMA((len(vals),))],
+        compiler_params=pltpu.CompilerParams(vmem_limit_bytes=2**20),
+        name='store',
+    )(*[pltpu.with_memory_space_constraint(val, pltpu.VMEM) for val in vals])
+
+
 def solution(mesh):
     def turn(val):
         return val.swapaxes(1, 2)
 
     def body(w_in, w_out, g_in, g_out, m_in, m_out, r_in, c_in, r_out, c_out, learn_rate, weight_decay, beta_two):
-        out = update_call((learn_rate, weight_decay, beta_two),
-                          (turn(w_in), w_out, turn(g_in[0]), g_out[0], m_in, turn(m_out), r_in, c_in, r_out, c_out))
+        out = store_call(update_call((learn_rate, weight_decay, beta_two),
+                          (turn(w_in), w_out, turn(g_in[0]), g_out[0], m_in, turn(m_out), r_in, c_in, r_out, c_out)))
         return (turn(out[0]), out[1], out[2], turn(out[3])) + tuple(out[4:])
 
     cols, rows, own = P(None, None, 'tp'), P(None, 'tp', None), P(None, 'dp')

time: 99.6 us -> 86.8 us (0.87)
  local copies, waits for them, and re-layouts: 7.41 us -> 0 us
  Pallas kernels: 89.4 us -> 84.1 us
    pallas_call x1, Pallas kernels: 89.4 us -> 80.8 us  [update_call(): pl.pallas_call(kernel, out_shape=[vmem(*out) for out in outs], in_specs=[...]
    unnamed x8 -> x0, local copies, waits for them, and re-layouts: 7.41 us -> none
    pallas_call x0 -> x1, Pallas kernels: none -> 3.21 us  [store_call(): pl.pallas_call(store_kernel, out_shape=[jax.ShapeDtypeStruct(val.shape, v...]
where the time goes in v2:
time: 86.8 us; the launch traced here: 86.6 us
  Pallas kernels  84.1 us (97%)
  between operations  2.58 us (3%)
    pallas_call x1, Pallas kernels, update_call(): pl.pallas_call(kernel, out_shape=[vmem(*out) for out in outs], in_specs=[...  80.8 us
    pallas_call x1, Pallas kernels, store_call(): pl.pallas_call(store_kernel, out_shape=[jax.ShapeDtypeStruct(val.shape, v...  3.21 us

profile of v2, /device:TPU:1, one launch (start us, length us, event | category | flops | bytes accessed | tf_op | source)
XLA Modules:
  0.0 86.6 jit_solution(7697331818107892799)
XLA Ops:
  2.6 80.8 %adafactor.1 = (f32[16,168,384]{2,1,0:T(8,128)S(1)}, f32[16,120,384]{2,1,0:T(8,128)S(1)}, bf16[16,48,168]{2,1,0:T(8,128)(2,1)S(1)}, bf16[16,48,120]{2,1,0:T(8,12...) custom-call(f32[1]{0:T(128)} %bitcast.11.rate_ref, ...), custom_call_target="tpu_custom_call" | custom-call | tf_op jit(solution)/shard_map/adafactor/pallas_call | solution.py:575
  83.4 3.2 %store.1 = (f32[16,168,384]{2,1,0:T(8,128)}, f32[16,120,384]{2,1,0:T(8,128)}, bf16[16,48,168]{2,1,0:T(8,128)(2,1)}, bf16[16,48,120]{2,1,0:T(8,128)(2,1)}, f32[16...) custom-call(f32[16,168,384]{2,1,0:T(8,128)S(1)} %get-tuple-element.24.refs_0_, ...), custom_call_target="tpu_custom_call" | custom-call | tf_op jit(solution)/shard_map/store/pallas_call | solution.py:597

commit v3 on v2

--- a/solution.py
+++ b/solution.py
@@ -14,8 +14,8 @@
 Q, LN, B48, B96 = 72, 128, 48, 96
 CH, HEAD, MID = 3 * Q, KI - 2 * Q, 256
 NI, KIN, NOUT, KO = 384.0, 2688.0, 1920.0, 384.0
-KINDS = RV, LY, LZ, SY, SZ, SX = range(6)
-AHEAD = 2
+KINDS = RV, SX, LT, ST = range(4)
+TP = RING * RING
 
 
 def roll(val, shift):
@@ -67,9 +67,9 @@
 def kernel(rate_ref, wd_ref, beta_ref, w_in, w_out, g_in, g_out, m_in, m_out, r_in, c_in, r_out, c_out,
            wn_in, wn_out, mn_in, mn_out, rn_in, cn_in, rn_out, cn_out,
            gbuf, pbuf, pack, via, rin, fin, mall, mraw_in, mraw_out, msend, mt, mpack, tall,
-           rvacc, lvacc, lraw, craw, oraw, pads, lvold, rvold, lvnew, rvnew, box_rv, box_ly, box_lz, box_sy, box_sz, box_sx,
+           rvacc, lvacc, lraw, craw, oraw, pads, lvold, rvold, lvnew, rvnew, box_rv, box_sx, box_lt, box_st,
            gl_sem, gs_sem, gr_sem, ml_sem, ms_sem, mr_sem, s_sem, via_sem, rin_sem, ags_sem, agr_sem,
-           shs_sem, shr_sem, sts_sem, str_sem, vs_sem, vr_sem, ol_sem, os_sem, or_sem, wl_sem):
+           shs_sem, shr_sem, sts_sem, str_sem, vs_sem, vr_sem, ol_sem, os_sem, wl_sem, ready):
     tp, dp = lax.axis_index('tp'), lax.axis_index('dp')
     z, y, x, c = tp // RING, tp % RING, dp // 2, dp % 2
     other = 1 - c
@@ -102,11 +102,11 @@
 
     def own(l, i):
         src, dst = ((g_in, first(KI)), (g_out, pl.ds(KI, NO)))[i]
-        return local(src.at[base + l], gbuf.at[l, dst], gl_sem.at[l, i])
+        return local(src.at[base + l], gbuf.at[l, dst], gl_sem.at[l // LG])
 
     def swap(l, i):
         src, dst = ((g_in, first(KI)), (g_out, pl.ds(KI, NO)))[i]
-        return remote(src.at[pbase + l], pbuf.at[l, dst], gs_sem.at[l, i], gr_sem.at[l, i], partner)
+        return remote(src.at[pbase + l], pbuf.at[l, dst], gs_sem.at[0], gr_sem.at[l // LG], partner)
 
     my_rows, its_rows = pl.ds(base, LC), pl.ds(pbase, LC)
     loads = [local(m_in, mraw_in, ml_sem.at[0]), local(m_out, mraw_out, ml_sem.at[1]),
@@ -115,7 +115,7 @@
     w_loads = [local(w_in, wn_in, wl_sem.at[0]), local(w_out, wn_out, wl_sem.at[1])]
 
     def lane_swap(m, core):
-        return remote((r_in, c_out)[m].at[its_rows], lraw.at[m, core], os_sem.at[m], or_sem.at[m], partner)
+        return remote((r_in, c_out)[m].at[its_rows], lraw.at[m, core], os_sem.at[0], os_sem.at[1], partner)
 
     def start_loads(l, carry):
         own(l, 0).start()
@@ -126,7 +126,9 @@
     for copy in loads:
         copy.start()
     pl.semaphore_wait(barrier, len(peers))
-    for l in range(AHEAD * LG):
+    for k in range(1, RING):
+        pl.semaphore_signal(ready, inc=1, device_id=at_y(y + k), device_id_type=MESH)
+    for l in range(LG):
         swap(l, 0).start()
         swap(l, 1).start()
     lane_swap(0, c).start()
@@ -151,25 +153,21 @@
     across = (x + 2) % RING
 
     def step1(l):
-        return remote(pack.at[l, across], via.at[l], s_sem.at[l, 0], via_sem.at[l], at_x(ahead(l)))
+        return remote(pack.at[l, across], via.at[l], s_sem.at[0], via_sem.at[l], at_x(ahead(l)))
 
     def step2(l):
-        return remote(pack.at[l, ahead(l)], rin.at[l, 0], s_sem.at[l, 1], rin_sem.at[l, 0], at_x(ahead(l)))
+        return remote(pack.at[l, ahead(l)], rin.at[l, 0], s_sem.at[0], rin_sem.at[l], at_x(ahead(l)))
 
     def step3(l):
-        return remote(pack.at[l, behind(l)], rin.at[l, 1], s_sem.at[l, 2], rin_sem.at[l, 1], at_x(behind(l)))
+        return remote(pack.at[l, behind(l)], rin.at[l, 1], s_sem.at[0], rin_sem.at[l], at_x(behind(l)))
 
     def m_rows(core):
         return pl.ds(pl.multiple_of(core * B48, 16), B48)
 
     def moment_swap(l, core):
-        return remote(msend.at[l], mt.at[l, m_rows(core)], ms_sem.at[l], mr_sem.at[l], partner)
+        return remote(msend.at[l], mt.at[l, m_rows(core)], ms_sem.at[0], mr_sem.at[l // LG], partner)
 
     def stage_a(l):
-        for i in range(2):
-            own(l, i).wait()
-            swap(l, i).wait_recv()
-
         def tile(t, q):
             return gbuf[l, block(q), tile_cols(t)] + pbuf[l, block(q), tile_cols(t)]
 
@@ -185,8 +183,6 @@
         for d in range(RING):
             for i, val in enumerate(join_quarters([chunk(d, q) for q in range(4)], m96)):
                 pack[l, d, block(i), :] = val
-        step1(l).start()
-        step3(l).start()
 
     def stage_n(l):
         msend[l, :, first(KI)] = mraw_in[pbase + l].astype(F32)
@@ -202,8 +198,7 @@
         step2(l).start()
 
     def stage_c(l):
-        step2(l).wait_recv()
-        step3(l).wait_recv()
+        remote(rin.at[l], rin.at[l], s_sem.at[0], rin_sem.at[l], partner).wait_recv()
         sq = []
         for i in range(3):
             grad = pack[l, x, block(i), :] + rin[l, 0, block(i), :] + rin[l, 1, block(i), :]
@@ -226,46 +221,45 @@
         lvacc[g] = jnp.where(row8 == LG + lg, out_sum, both)
 
     def stage_m(l):
-        moment_swap(l, other).wait_recv()
         val = mt[l].T
         third = jnp.concatenate([val[2 * Q:KI], val[MID:MID + B48]], axis=0)
         quarters = [val[:Q], val[Q:2 * Q], third, val[MID + B48:MID + NO]]
         for i, part in enumerate(join_quarters(quarters, m96)):
             mpack[l, block(i), :] = part
 
-    boxes = {RV: (box_rv, x, at_x), LY: (box_ly, y, at_y), LZ: (box_lz, z, at_z),
-             SX: (box_sx, x, at_x), SY: (box_sy, y, at_y), SZ: (box_sz, z, at_z)}
-
-    def box_copy(kind, g, k, slot):
-        box, me, place = boxes[kind]
-        return remote(box.at[g, slot], box.at[g, slot], sts_sem.at[g, kind, k - 1], str_sem.at[g, kind, slot], place(me + k))
+    boxes = {RV: (box_rv, x, RING), SX: (box_sx, x, RING), LT: (box_lt, tp, TP), ST: (box_st, tp, TP)}
 
     def post(kind, g, val):
-        box, me, place = boxes[kind]
+        box, me, num = boxes[kind]
         box[g, me] = val
-        for k in range(1, RING):
-            box_copy(kind, g, k, me).start()
+
+        def send(k, carry):
+            device = at_x(me + k) if num == RING else {'tp': (me + k) % TP}
+            remote(box.at[g, me], box.at[g, me], sts_sem.at[0], str_sem.at[g, kind], device).start()
+            return carry
+
+        lax.fori_loop(1, num, send, 0)
 
     def collect(kind, g):
-        box, me, place = boxes[kind]
-        for k in range(1, RING):
-            box_copy(kind, g, k, (me + k) % RING).wait_recv()
-        return ((box[g, 0] + box[g, 1]) + box[g, 2]) + box[g, 3]
+        box, me, num = boxes[kind]
+        rest = box.at[g, first(num - 1)]
+        remote(rest, rest, sts_sem.at[0], str_sem.at[g, kind], partner).wait_recv()
+        val = box[g, 0]
+        for k in range(1, num):
+            val = val + box[g, k]
+        return val
 
     def sums_send(g):
-        post(LY, g, lvacc[g])
+        post(LT, g, lvacc[g])
         post(RV, g, rvacc[g].T[:8])
-
-    def sums_mid(g):
-        post(LZ, g, collect(LY, g))
 
     beta = beta_ref[0]
 
     def old_vectors():
         for copy in loads[2:]:
             copy.wait()
+        remote(lraw.at[0], lraw.at[0], os_sem.at[0], os_sem.at[1], partner).wait_recv()
         for m in range(2):
-            lane_swap(m, other).wait_recv()
             for core in range(2):
                 pads[m, core, :, first(B48)] = lraw[m, core]
         pads[2, 0, :, first(KI - LN)] = craw[:, pl.ds(LN, KI - LN)]
@@ -281,10 +275,10 @@
 
     def vec_swap(g, half, i):
         ref = (lvnew, rvnew)[i]
-        return remote(ref.at[half, g], ref.at[half, g], vs_sem.at[g, i], vr_sem.at[g, i], partner)
+        return remote(ref.at[half, g], ref.at[half, g], vs_sem.at[0], vr_sem.at[i], partner)
 
     def moments(g):
-        lv_mean = collect(LZ, g) / jnp.where(row8 < LG, KIN, NOUT)
+        lv_mean = collect(LT, g) / jnp.where(row8 < LG, KIN, NOUT)
         lv_new = beta * lvold[g] + (1.0 - beta) * lv_mean
         lvnew[c, g] = lv_new
         rv_new = beta * rvold[g] + (1.0 - beta) * (collect(RV, g) / NI)
@@ -314,13 +308,10 @@
             v_out = pick((lane1 >= HEAD) & (lane1 < Q), rv_new[2 * LG + lg:2 * LG + lg + 1, :]) + pick(lane1 < Q, rv_new[3 * LG + lg:3 * LG + lg + 1, :])
             for k, val in enumerate((colsum(inner), colsum(outer), v_in, v_out)):
                 tots = jnp.where(row8 == LG * k + lg, val, tots)
-        post(SY, g, tots)
-
-    def totals_y(g):
-        post(SZ, g, jnp.where(only_x, box_sy[g, y], collect(SY, g)))
-
-    def totals_z(g):
-        post(SX, g, jnp.where(only_x, box_sz[g, z], collect(SZ, g)))
+        post(ST, g, tots)
+
+    def totals(g):
+        post(SX, g, jnp.where(only_x, box_st[g, tp], collect(ST, g)))
 
     def factors(g):
         tot = rowsum(jnp.where(no_x, box_sx[g, x], collect(SX, g)))
@@ -339,19 +330,17 @@
     def gather(l, k):
         slot = x if k < 2 else behind(l)
         ref = mall.at[base + l, slot]
-        return remote(ref, ref, ags_sem.at[l, k], agr_sem.at[l, k], at_x(behind(l) if k == 1 else ahead(l)))
-
-    def arrival(l, k):
-        ref = mall.at[base + l, (behind(l), ahead(l), across)[k]]
-        return remote(ref, ref, ags_sem.at[l, k], agr_sem.at[l, k], at_x(ahead(l)))
+        return remote(ref, ref, ags_sem.at[0], agr_sem.at[l, min(k, 1)], at_x(behind(l) if k == 1 else ahead(l)))
 
     def share(l, k, start):
         ref = mall.at[start + l, (behind(l), ahead(l), across, x)[k]]
-        return remote(ref, ref, shs_sem.at[l, k], shr_sem.at[l, k], partner)
+        return remote(ref, ref, shs_sem.at[0], shr_sem.at[l], partner)
 
     def send_pair(l):
         gather(l, 0).start()
         gather(l + 1, 0).start()
+
+    def send_back(l):
         gather(l, 1).start()
         gather(l + 1, 1).start()
         share(l, 3, base).start()
@@ -359,14 +348,15 @@
 
     def forward_pair(l):
         for k in (l, l + 1):
-            arrival(k, 0).wait_recv()
+            gather(k, 0).wait_recv()
             gather(k, 2).start()
             share(k, 0, base).start()
 
     def settle_pair(l):
         for k in (l, l + 1):
+            two = mall.at[base + k, first(2)]
+            remote(two, two, ags_sem.at[0], agr_sem.at[k, 1], partner).wait_recv()
             for i in (1, 2):
-                arrival(k, i).wait_recv()
                 share(k, i, base).start()
 
     rate = rate_ref[0]
@@ -403,8 +393,8 @@
 
     def take_pair(l):
         for k in (l, l + 1):
-            for i in range(4):
-                share(k, i, pbase).wait_recv()
+            four = mall.at[pbase + k]
+            remote(four, four, shs_sem.at[0], shr_sem.at[k], partner).wait_recv()
         unpack_pair(l, pbase)
 
     def new_vectors():
@@ -422,134 +412,113 @@
                 rn_out[rows, :] = jnp.where(lane4 < B48, roll(val, -HEAD)[2 * LG:3 * LG], roll(val, B48)[3 * LG:])[:, :NO]
 
     def both(step, g):
-        for lg in range(LG):
-            step(LG * g + lg)
+        lax.fori_loop(LG * g, LG * g + LG, lambda l, carry: (step(l), carry)[1], 0)
 
     def swap_start(l):
         swap(l, 0).start()
         swap(l, 1).start()
 
-    def stage(it, carry):
-        @pl.when(it < NG)
-        def _():
-            both(stage_a, it)
-
-        @pl.when(it < NG - AHEAD)
-        def _():
-            both(swap_start, it + AHEAD)
-
-        @pl.when(it == 0)
-        def _():
+    def pack_pair(g):
+        two = pl.ds(LG * g, LG)
+        local(gbuf.at[two], gbuf.at[two], gl_sem.at[g]).wait()
+        remote(pbuf.at[two], pbuf.at[two], gs_sem.at[0], gr_sem.at[g], partner).wait_recv()
+        if g + 1 < NG:
+            both(swap_start, g + 1)
+        both(stage_a, g)
+        both(lambda l: step1(l).start(), g)
+
+    def rest_pair(g):
+        both(lambda l: step3(l).start(), g)
+        if g == 0:
             loads[0].wait()
             loads[1].wait()
-
-        @pl.when((it >= 1) & (it <= NG))
-        def _():
-            both(stage_b, it - 1)
-
-        @pl.when(it == 4)
-        def _():
-            totals_y(0)
-
-        @pl.when((it == 3) | (it == 4))
-        def _():
-            sums_mid(it - 3)
-
-        @pl.when(it < NG)
-        def _():
-            both(stage_n, it)
-
-        @pl.when(it == 2)
-        def _():
-            w_loads[0].start()
-            w_loads[1].start()
-            old_vectors()
-
-        @pl.when(it >= 2)
-        def _():
-            both(stage_c, it - 2)
-            sums_send(it - 2)
-            both(stage_m, it - 2)
-
-        @pl.when(it == 4)
-        def _():
-            totals_z(0)
-
-        @pl.when((it == 3) | (it == 4))
-        def _():
-            moments(it - 3)
-
-        return carry
-
-    lax.fori_loop(0, NG + 2, stage, 0)
+        both(stage_n, g)
+
+    def relay_pair(g):
+        both(stage_b, g)
+
+    def sum_pair(g):
+        both(stage_c, g)
+        sums_send(g)
+
+    def moment_pair(g):
+        two = msend.at[pl.ds(LG * g, LG)]
+        remote(two, two, ms_sem.at[0], mr_sem.at[g], partner).wait_recv()
+        both(stage_m, g)
 
     def update_pair(g):
         fac = factors(g)
         for lg in range(LG):
             update(LG * g + lg, lg, fac)
 
+    pack_pair(0)
+    rest_pair(0)
+    pack_pair(1)
+    w_loads[0].start()
+    w_loads[1].start()
+    old_vectors()
+    pl.semaphore_wait(ready, RING - 1)
+    relay_pair(0)
+    rest_pair(1)
+    pack_pair(2)
+    sum_pair(0)
+    relay_pair(1)
+    rest_pair(2)
+    moment_pair(0)
+    pack_pair(3)
+    moments(0)
+    sum_pair(1)
+    relay_pair(2)
+    rest_pair(3)
+    moment_pair(1)
+    totals(0)
+    relay_pair(3)
+    moments(1)
+    sum_pair(2)
+    moment_pair(2)
     update_pair(0)
     send_pair(0)
-    totals_y(1)
-    sums_mid(2)
-    totals_z(1)
+    totals(1)
+    send_back(0)
+    sum_pair(3)
+    moment_pair(3)
     moments(2)
-    sums_mid(3)
     forward_pair(0)
     update_pair(1)
     send_pair(2)
-    totals_y(2)
     moments(3)
-    totals_z(2)
-    totals_y(3)
+    totals(2)
+    send_back(2)
     settle_pair(0)
-    forward_pair(2)
     w_loads[0].wait()
     w_loads[1].wait()
     unpack_pair(0, base)
-    totals_z(3)
+    forward_pair(2)
+    totals(3)
     update_pair(2)
     send_pair(4)
+    send_back(4)
     take_pair(0)
     settle_pair(2)
     update_pair(3)
+    send_pair(6)
     forward_pair(4)
-    send_pair(6)
+    send_back(6)
     unpack_pair(2, base)
     take_pair(2)
-    for g in range(NG):
-        for i in range(2):
-            vec_swap(g, other, i).wait_recv()
+    for i, ref in enumerate((lvnew, rvnew)):
+        remote(ref.at[other], ref.at[other], vs_sem.at[0], vr_sem.at[i], partner).wait_recv()
     new_vectors()
+    forward_pair(6)
     settle_pair(4)
     unpack_pair(4, base)
-    forward_pair(6)
     take_pair(4)
     settle_pair(6)
     unpack_pair(6, base)
     take_pair(6)
-
-    def drain(l, carry):
-        for i in range(2):
-            swap(l, i).wait_send()
-        moment_swap(l, c).wait_send()
-        for step in (step1, step2, step3):
-            step(l).wait_send()
-        for k in range(3):
-            gather(l, k).wait_send()
-        for k in range(4):
-            share(l, k, base).wait_send()
-        return carry
-
-    lax.fori_loop(0, LC, drain, 0)
-    for m in range(2):
-        lane_swap(m, c).wait_send()
-    for g in range(NG):
-        for kind in KINDS:
-            for k in range(1, RING):
-                box_copy(kind, g, k, boxes[kind][1]).wait_send()
-        for i in range(2):
-            vec_swap(g, c, i).wait_send()
+    for ref, sem in ((pbuf, gs_sem), (msend, ms_sem), (mall.at[first(6)], s_sem), (mall.at[first(6)], ags_sem), (mall.at[first(8)], shs_sem),
+                     (lraw.at[0], os_sem), (mt.at[first(3)], sts_sem), (lvnew, vs_sem)):
+        remote(ref, ref, sem.at[0], os_sem.at[1], partner).wait_send()
 
 
 def update_call(scalars, arrays):
@@ -565,10 +534,9 @@
         lanes(LC, CH), lanes(D), lanes(NG, LN), lanes(NG, 8),
         vmem((2, 2, LC, B48), F32), vmem((LC, KI), F32), vmem((LC, NO), F32), lanes(3, 2, LC),
         lanes(NG, 8), lanes(NG, 8), lanes(2, NG, 8), lanes(2, NG, 8),
-        *[lanes(NG, RING, 8)] * len(KINDS),
-        dma((LC, 2)), dma((LC, 2)), dma((LC, 2)), dma((2,)), dma((LC,)), dma((LC,)), dma((LC, 3)), dma((LC,)), dma((LC, 2)),
-        dma((LC, 3)), dma((LC, 3)), dma((LC, 4)), dma((LC, 4)), dma((NG, len(KINDS), 3)), dma((NG, len(KINDS), RING)),
-        dma((NG, 2)), dma((NG, 2)), dma((4,)), dma((2,)), dma((2,)), dma((2,)),
+        lanes(NG, RING, 8), lanes(NG, RING, 8), lanes(NG, TP, 8), lanes(NG, TP, 8),
+        dma((NG,)), dma((1,)), dma((NG,)), dma((2,)), dma((1,)), dma((NG,)), dma((1,)), dma((LC,)), dma((LC,)), dma((1,)), dma((LC, 2)),
+        dma((1,)), dma((LC,)), dma((1,)), dma((NG, len(KINDS))), dma((1,)), dma((2,)), dma((4,)), dma((2,)), dma((2,)), pltpu.SemaphoreType.REGULAR,
     ]
     outs = [((L, KI, D), F32), ((L, NO, D), F32), ((L, B48, KI), BF16), ((L, B48, NO), BF16),
             ((L, B48), F32), ((L, KI), F32), ((L, NO), F32), ((L, B48), F32)]

time: 86.8 us -> 79.8 us (0.919)
  Pallas kernels: 84.1 us -> 77.1 us
    pallas_call x1, Pallas kernels: 80.8 us -> 73.9 us  [update_call(): pl.pallas_call(kernel, out_shape=[vmem(*out) for out in outs], in_specs=[...]
where the time goes in v3:
time: 79.8 us; the launch traced here: 79.6 us
  Pallas kernels  77.1 us (97%)
  between operations  2.58 us (3%)
    pallas_call x1, Pallas kernels, update_call(): pl.pallas_call(kernel, out_shape=[vmem(*out) for out in outs], in_specs=[...  73.9 us
    pallas_call x1, Pallas kernels, store_call(): pl.pallas_call(store_kernel, out_shape=[jax.ShapeDtypeStruct(val.shape, v...  3.21 us

profile of v3, /device:TPU:1, one launch (start us, length us, event | category | flops | bytes accessed | tf_op | source)
XLA Modules:
  0.0 79.6 jit_solution(13109766505464921419)
XLA Ops:
  2.6 73.9 %adafactor.1 = (f32[16,168,384]{2,1,0:T(8,128)S(1)}, f32[16,120,384]{2,1,0:T(8,128)S(1)}, bf16[16,48,168]{2,1,0:T(8,128)(2,1)S(1)}, bf16[16,48,120]{2,1,0:T(8,12...) custom-call(f32[1]{0:T(128)} %bitcast.11.rate_ref, ...), custom_call_target="tpu_custom_call" | custom-call | tf_op jit(solution)/shard_map/adafactor/pallas_call | solution.py:543
  76.4 3.2 %store.1 = (f32[16,168,384]{2,1,0:T(8,128)}, f32[16,120,384]{2,1,0:T(8,128)}, bf16[16,48,168]{2,1,0:T(8,128)(2,1)}, bf16[16,48,120]{2,1,0:T(8,128)(2,1)}, f32[16...) custom-call(f32[16,168,384]{2,1,0:T(8,128)S(1)} %get-tuple-element.24.refs_0_, ...), custom_call_target="tpu_custom_call" | custom-call | tf_op jit(solution)/shard_map/store/pallas_call | solution.py:565

commit v4 on v3

--- a/solution.py
+++ b/solution.py
@@ -12,7 +12,7 @@
 KI, NO = 168, 120
 LC, LG, NG = 8, 2, 4
 Q, LN, B48, B96 = 72, 128, 48, 96
-CH, HEAD, MID = 3 * Q, KI - 2 * Q, 256
+CH, HEAD, MID, HALF = 3 * Q, KI - 2 * Q, 256, 104
 NI, KIN, NOUT, KO = 384.0, 2688.0, 1920.0, 384.0
 KINDS = RV, SX, LT, ST = range(4)
 TP = RING * RING
@@ -66,9 +66,9 @@
 
 def kernel(rate_ref, wd_ref, beta_ref, w_in, w_out, g_in, g_out, m_in, m_out, r_in, c_in, r_out, c_out,
            wn_in, wn_out, mn_in, mn_out, rn_in, cn_in, rn_out, cn_out,
-           gbuf, pbuf, pack, via, rin, fin, mall, mraw_in, mraw_out, msend, mt, mpack, tall,
+           gbuf, pbuf, gsend, pack, via, rin, fin, mall, mraw_in, mraw_out, msend, mt, mpack, tall,
            rvacc, lvacc, lraw, craw, oraw, pads, lvold, rvold, lvnew, rvnew, box_rv, box_sx, box_lt, box_st,
-           gl_sem, gs_sem, gr_sem, ml_sem, ms_sem, mr_sem, s_sem, via_sem, rin_sem, ags_sem, agr_sem,
+           gl_sem, gp_sem, gs_sem, gr_sem, ml_sem, ms_sem, mr_sem, s_sem, via_sem, rin_sem, ags_sem, agr_sem,
            shs_sem, shr_sem, sts_sem, str_sem, vs_sem, vr_sem, ol_sem, os_sem, wl_sem, ready):
     tp, dp = lax.axis_index('tp'), lax.axis_index('dp')
     z, y, x, c = tp // RING, tp % RING, dp // 2, dp % 2
@@ -102,7 +102,14 @@
 
     def own(l, i):
         src, dst = ((g_in, first(KI)), (g_out, pl.ds(KI, NO)))[i]
-        return local(src.at[base + l], gbuf.at[l, dst], gl_sem.at[l // LG])
+        return local(src.at[base + l], gbuf.at[l, dst], gl_sem.at[NG + l] if isinstance(l, int) else gl_sem.at[l // LG])
+
+    def others(l, i):
+        src, dst = ((g_in, first(KI)), (g_out, pl.ds(KI, NO)))[i]
+        return local(src.at[pbase + l], gsend.at[l, dst], gp_sem.at[l])
+
+    def swap_first(l):
+        return remote(gsend.at[l], pbuf.at[l], gs_sem.at[0], gr_sem.at[NG + l], partner)
 
     def swap(l, i):
         src, dst = ((g_in, first(KI)), (g_out, pl.ds(KI, NO)))[i]
@@ -122,15 +129,19 @@
         own(l, 1).start()
         return carry
 
-    lax.fori_loop(0, LC, start_loads, 0)
+    for l in range(LG):
+        for i in range(2):
+            others(l, i).start()
+            own(l, i).start()
+    lax.fori_loop(LG, LC, start_loads, 0)
     for copy in loads:
         copy.start()
     pl.semaphore_wait(barrier, len(peers))
     for k in range(1, RING):
         pl.semaphore_signal(ready, inc=1, device_id=at_y(y + k), device_id_type=MESH)
     for l in range(LG):
-        swap(l, 0).start()
-        swap(l, 1).start()
+        local(gsend.at[l], gsend.at[l], gp_sem.at[l]).wait()
+        swap_first(l).start()
     lane_swap(0, c).start()
     lane_swap(1, c).start()
     rvacc[...] = jnp.zeros_like(rvacc)
@@ -156,10 +167,10 @@
         return remote(pack.at[l, across], via.at[l], s_sem.at[0], via_sem.at[l], at_x(ahead(l)))
 
     def step2(l):
-        return remote(pack.at[l, ahead(l)], rin.at[l, 0], s_sem.at[0], rin_sem.at[l], at_x(ahead(l)))
+        return remote(pack.at[l, ahead(l)], rin.at[l, 0], s_sem.at[0], rin_sem.at[l // LG], at_x(ahead(l)))
 
     def step3(l):
-        return remote(pack.at[l, behind(l)], rin.at[l, 1], s_sem.at[0], rin_sem.at[l], at_x(behind(l)))
+        return remote(pack.at[l, behind(l)], rin.at[l, 1], s_sem.at[0], rin_sem.at[l // LG], at_x(behind(l)))
 
     def m_rows(core):
         return pl.ds(pl.multiple_of(core * B48, 16), B48)
@@ -198,7 +209,6 @@
         step2(l).start()
 
     def stage_c(l):
-        remote(rin.at[l], rin.at[l], s_sem.at[0], rin_sem.at[l], partner).wait_recv()
         sq = []
         for i in range(3):
             grad = pack[l, x, block(i), :] + rin[l, 0, block(i), :] + rin[l, 1, block(i), :]
@@ -327,14 +337,17 @@
             new = 0.9 * mpack[l, block(i), :] + 0.1 * upd
             mall[base + l, x, block(i), :] = new.astype(BF16).astype(F32)
 
+    def arrived(l, k):
+        return l if k == 0 else LC + NG if k == 1 and l >= LC - LG else LC + l // LG
+
     def gather(l, k):
         slot = x if k < 2 else behind(l)
         ref = mall.at[base + l, slot]
-        return remote(ref, ref, ags_sem.at[0], agr_sem.at[l, min(k, 1)], at_x(behind(l) if k == 1 else ahead(l)))
+        return remote(ref, ref, ags_sem.at[0], agr_sem.at[arrived(l, k)], at_x(behind(l) if k == 1 else ahead(l)))
 
     def share(l, k, start):
         ref = mall.at[start + l, (behind(l), ahead(l), across, x)[k]]
-        return remote(ref, ref, shs_sem.at[0], shr_sem.at[l], partner)
+        return remote(ref, ref, shs_sem.at[0], shr_sem.at[NG if k == 3 and l >= LC - LG else l // LG], partner)
 
     def send_pair(l):
         gather(l, 0).start()
@@ -352,12 +365,40 @@
             gather(k, 2).start()
             share(k, 0, base).start()
 
+    def half(ref, h):
+        return ref.at[(first(HALF), pl.ds(HALF, CH - HALF))[h]]
+
+    def gather_half(l, h, slot):
+        ref = half(mall.at[base + l, slot], h)
+        return remote(ref, ref, ags_sem.at[0], agr_sem.at[l if h == 0 else LC + NG + 1 + l], at_x(ahead(l)))
+
+    def send_first():
+        for h in range(2):
+            for l in range(LG):
+                gather_half(l, h, x).start()
+
+    def forward_first():
+        for h in range(2):
+            for l in range(LG):
+                gather_half(l, h, behind(l)).wait_recv()
+                ref = half(mall.at[base + l, behind(l)], h)
+                remote(ref, ref, ags_sem.at[0], agr_sem.at[arrived(l, 2)], at_x(ahead(l))).start()
+        share(0, 0, base).start()
+        share(1, 0, base).start()
+
     def settle_pair(l):
+        four = mall.at[base + l]
+        remote(four, four, ags_sem.at[0], agr_sem.at[LC + l // LG], partner).wait_recv()
         for k in (l, l + 1):
-            two = mall.at[base + k, first(2)]
-            remote(two, two, ags_sem.at[0], agr_sem.at[k, 1], partner).wait_recv()
             for i in (1, 2):
                 share(k, i, base).start()
+
+    def settle_last(k):
+        l = LC - LG
+        two = mall.at[base + l, first(LG)]
+        remote(two, two, ags_sem.at[0], agr_sem.at[arrived(l, k)], partner).wait_recv()
+        share(l, k, base).start()
+        share(l + 1, k, base).start()
 
     rate = rate_ref[0]
     decay = rate * wd_ref[0]
@@ -376,6 +417,8 @@
                     rows = pl.ds(dst, num)
                     w = ref[at, rows, tile_cols(t)]
                     ref[at, rows, tile_cols(t)] = w - rate * mom[t][src:src + num] - decay * w
+
+    def turn_moment(at):
         parts = [mall[at, x, block(i), :] for i in range(3)]
         parts.append(last_quarter(parts))
         spots = ((0, 0, Q),), ((Q, 0, Q),), ((2 * Q, 0, HEAD), (MID, HEAD, B48)), ((MID + B48, 0, Q),)
@@ -388,13 +431,24 @@
         mn_in[at, :, pl.ds(LN, KI - LN)] = turned[1][:, :KI - LN].astype(BF16)
         mn_out[at] = turned[2][:, :NO].astype(BF16)
 
+    def each(step, l, start):
+        lax.fori_loop(start + l, start + l + LG, lambda at, carry: (step(at), carry)[1], 0)
+
     def unpack_pair(l, start):
-        lax.fori_loop(start + l, start + l + 2, lambda at, carry: (unpack(at), carry)[1], 0)
+        each(unpack, l, start)
+        if l < LC - LG:
+            each(turn_moment, l, start)
+
+    def turn_last():
+        l = LC - LG
+        each(turn_moment, l, base)
+        two = mall.at[base, first(LG)]
+        remote(two, two, shs_sem.at[0], shr_sem.at[NG], partner).wait_recv()
+        each(turn_moment, l, pbase)
 
     def take_pair(l):
-        for k in (l, l + 1):
-            four = mall.at[pbase + k]
-            remote(four, four, shs_sem.at[0], shr_sem.at[k], partner).wait_recv()
+        two = mall.at[pl.ds(pbase + l, LG)] if l < LC - LG else mall.at[pl.ds(pbase + l, LG), first(3)]
+        remote(two, two, shs_sem.at[0], shr_sem.at[l // LG], partner).wait_recv()
         unpack_pair(l, pbase)
 
     def new_vectors():
@@ -418,6 +472,16 @@
         swap(l, 0).start()
         swap(l, 1).start()
 
+    def pack_first():
+        for l in range(LG):
+            local(gbuf.at[l], gbuf.at[l], gl_sem.at[NG + l]).wait()
+            swap_first(l).wait_recv()
+            stage_a(l)
+            step1(l).start()
+            if l == 0:
+                both(swap_start, 1)
+        both(lambda l: step3(l).start(), 0)
+
     def pack_pair(g):
         two = pl.ds(LG * g, LG)
         local(gbuf.at[two], gbuf.at[two], gl_sem.at[g]).wait()
@@ -427,8 +491,10 @@
         both(stage_a, g)
         both(lambda l: step1(l).start(), g)
 
-    def rest_pair(g):
+    def direct_pair(g):
         both(lambda l: step3(l).start(), g)
+
+    def cast_pair(g):
         if g == 0:
             loads[0].wait()
             loads[1].wait()
@@ -438,6 +504,8 @@
         both(stage_b, g)
 
     def sum_pair(g):
+        two = rin.at[pl.ds(LG * g, LG)]
+        remote(two, two, s_sem.at[0], rin_sem.at[g], partner).wait_recv()
         both(stage_c, g)
         sums_send(g)
 
@@ -451,53 +519,56 @@
         for lg in range(LG):
             update(LG * g + lg, lg, fac)
 
-    pack_pair(0)
-    rest_pair(0)
+    pack_first()
+    cast_pair(0)
     pack_pair(1)
     w_loads[0].start()
     w_loads[1].start()
     old_vectors()
     pl.semaphore_wait(ready, RING - 1)
     relay_pair(0)
-    rest_pair(1)
+    direct_pair(1)
+    cast_pair(1)
     pack_pair(2)
     sum_pair(0)
     relay_pair(1)
-    rest_pair(2)
+    direct_pair(2)
+    cast_pair(2)
     moment_pair(0)
     pack_pair(3)
     moments(0)
     sum_pair(1)
     relay_pair(2)
-    rest_pair(3)
+    cast_pair(3)
     moment_pair(1)
     totals(0)
+    direct_pair(3)
     relay_pair(3)
     moments(1)
     sum_pair(2)
     moment_pair(2)
     update_pair(0)
-    send_pair(0)
+    send_first()
     totals(1)
     send_back(0)
     sum_pair(3)
     moment_pair(3)
     moments(2)
-    forward_pair(0)
+    forward_first()
     update_pair(1)
     send_pair(2)
     moments(3)
     totals(2)
     send_back(2)
+    forward_pair(2)
     settle_pair(0)
-    w_loads[0].wait()
-    w_loads[1].wait()
-    unpack_pair(0, base)
-    forward_pair(2)
     totals(3)
     update_pair(2)
     send_pair(4)
     send_back(4)
+    w_loads[0].wait()
+    w_loads[1].wait()
+    unpack_pair(0, base)
     take_pair(0)
     settle_pair(2)
     update_pair(3)
@@ -509,11 +580,13 @@
     for i, ref in enumerate((lvnew, rvnew)):
         remote(ref.at[other], ref.at[other], vs_sem.at[0], vr_sem.at[i], partner).wait_recv()
     new_vectors()
+    turn_last()
     forward_pair(6)
     settle_pair(4)
     unpack_pair(4, base)
+    settle_last(1)
     take_pair(4)
-    settle_pair(6)
+    settle_last(2)
     unpack_pair(6, base)
     take_pair(6)
     for ref, sem in ((pbuf, gs_sem), (msend, ms_sem), (mall.at[first(6)], s_sem), (mall.at[first(6)], ags_sem), (mall.at[first(8)], shs_sem),
@@ -529,14 +602,15 @@
         return vmem(lead + (LN,), F32)
 
     scratch = [
-        vmem((LC, KI + NO, D), F32), vmem((LC, KI + NO, D), F32), lanes(LC, RING, CH), lanes(LC, CH), lanes(LC, 2, CH), lanes(LC, CH),
+        vmem((LC, KI + NO, D), F32), vmem((LC, KI + NO, D), F32), vmem((LG, KI + NO, D), F32), lanes(LC, RING, CH), lanes(LC, CH), lanes(LC, 2, CH), lanes(LC, CH),
         lanes(L, RING, CH), vmem((L, B48, KI), BF16), vmem((L, B48, NO), BF16), vmem((LC, B48, D), F32), vmem((LC, LN, D), F32),
         lanes(LC, CH), lanes(D), lanes(NG, LN), lanes(NG, 8),
         vmem((2, 2, LC, B48), F32), vmem((LC, KI), F32), vmem((LC, NO), F32), lanes(3, 2, LC),
         lanes(NG, 8), lanes(NG, 8), lanes(2, NG, 8), lanes(2, NG, 8),
         lanes(NG, RING, 8), lanes(NG, RING, 8), lanes(NG, TP, 8), lanes(NG, TP, 8),
-        dma((NG,)), dma((1,)), dma((NG,)), dma((2,)), dma((1,)), dma((NG,)), dma((1,)), dma((LC,)), dma((LC,)), dma((1,)), dma((LC, 2)),
-        dma((1,)), dma((LC,)), dma((1,)), dma((NG, len(KINDS))), dma((1,)), dma((2,)), dma((4,)), dma((2,)), dma((2,)), pltpu.SemaphoreType.REGULAR,
+        dma((NG + LG,)), dma((LG,)), dma((1,)), dma((NG + LG,)), dma((2,)), dma((1,)), dma((NG,)), dma((1,)), dma((LC,)), dma((NG,)),
+        dma((1,)), dma((LC + NG + 1 + LG,)), dma((1,)), dma((NG + 1,)), dma((1,)), dma((NG, len(KINDS))), dma((1,)), dma((2,)), dma((4,)),
+        dma((2,)), dma((2,)), pltpu.SemaphoreType.REGULAR,
     ]
     outs = [((L, KI, D), F32), ((L, NO, D), F32), ((L, B48, KI), BF16), ((L, B48, NO), BF16),
             ((L, B48), F32), ((L, KI), F32), ((L, NO), F32), ((L, B48), F32)]

time: 79.8 us -> 78.3 us (0.981)
  Pallas kernels: 77.1 us -> 75.6 us
    pallas_call x1, Pallas kernels: 73.9 us -> 72.4 us  [update_call(): pl.pallas_call(kernel, out_shape=[vmem(*out) for out in outs], in_specs=[...]
where the time goes in v4:
time: 78.3 us; the launch traced here: 78.2 us
  Pallas kernels  75.6 us (97%)
  between operations  2.58 us (3%)
    pallas_call x1, Pallas kernels, update_call(): pl.pallas_call(kernel, out_shape=[vmem(*out) for out in outs], in_specs=[...  72.4 us
    pallas_call x1, Pallas kernels, store_call(): pl.pallas_call(store_kernel, out_shape=[jax.ShapeDtypeStruct(val.shape, v...  3.21 us

profile of v4, /device:TPU:1, one launch (start us, length us, event | category | flops | bytes accessed | tf_op | source)
XLA Modules:
  0.0 78.2 jit_solution(3346920180998555637)
XLA Ops:
  2.6 72.4 %adafactor.1 = (f32[16,168,384]{2,1,0:T(8,128)S(1)}, f32[16,120,384]{2,1,0:T(8,128)S(1)}, bf16[16,48,168]{2,1,0:T(8,128)(2,1)S(1)}, bf16[16,48,120]{2,1,0:T(8,12...) custom-call(f32[1]{0:T(128)} %bitcast.11.rate_ref, ...), custom_call_target="tpu_custom_call" | custom-call | tf_op jit(solution)/shard_map/adafactor/pallas_call | solution.py:617
  75.0 3.2 %store.1 = (f32[16,168,384]{2,1,0:T(8,128)}, f32[16,120,384]{2,1,0:T(8,128)}, bf16[16,48,168]{2,1,0:T(8,128)(2,1)}, bf16[16,48,120]{2,1,0:T(8,128)(2,1)}, f32[16...) custom-call(f32[16,168,384]{2,1,0:T(8,128)S(1)} %get-tuple-element.24.refs_0_, ...), custom_call_target="tpu_custom_call" | custom-call | tf_op jit(solution)/shard_map/store/pallas_call | solution.py:639

commit v5 on v4

--- a/solution.py
+++ b/solution.py
@@ -150,7 +150,7 @@
     lane, lane8, row8 = lane_of((Q, LN)), lane_of((8, LN)), row_of((8, LN))
     m96, k96 = lane < B96, lane8 < B96
     head = row_of((Q, LN)) < HEAD
-    no_x, only_x = row8 >= 3 * LG, (row8 >= 2 * LG) & (row8 < 3 * LG)
+    only_x = (row8 >= 2 * LG) & (row8 < 3 * LG)
 
     def way(l):
         return 1 - 2 * (l % 2)
@@ -191,9 +191,20 @@
                 return roll(jnp.where(lane < 64, tile(2, q), tile(1, q)), 64)
             return roll(tile(2, q), B96)
 
-        for d in range(RING):
+        def put(d):
             for i, val in enumerate(join_quarters([chunk(d, q) for q in range(4)], m96)):
                 pack[l, d, block(i), :] = val
+
+        if not isinstance(l, int):
+            for d in range(RING):
+                put(d)
+            return
+
+        for d in range(RING):
+            pl.when(across == d)(lambda: put(d))
+        step1(l).start()
+        for d in range(RING):
+            pl.when(across != d)(lambda: put(d))
 
     def stage_n(l):
         msend[l, :, first(KI)] = mraw_in[pbase + l].astype(F32)
@@ -245,7 +256,7 @@
 
         def send(k, carry):
             device = at_x(me + k) if num == RING else {'tp': (me + k) % TP}
-            remote(box.at[g, me], box.at[g, me], sts_sem.at[0], str_sem.at[g, kind], device).start()
+            remote(box.at[g, me], box.at[g, me], sts_sem.at[int(kind == SX)], str_sem.at[g, kind], device).start()
             return carry
 
         lax.fori_loop(1, num, send, 0)
@@ -253,7 +264,7 @@
     def collect(kind, g):
         box, me, num = boxes[kind]
         rest = box.at[g, first(num - 1)]
-        remote(rest, rest, sts_sem.at[0], str_sem.at[g, kind], partner).wait_recv()
+        remote(rest, rest, sts_sem.at[int(kind == SX)], str_sem.at[g, kind], partner).wait_recv()
         val = box[g, 0]
         for k in range(1, num):
             val = val + box[g, k]
@@ -321,10 +332,12 @@
         post(ST, g, tots)
 
     def totals(g):
-        post(SX, g, jnp.where(only_x, box_st[g, tp], collect(ST, g)))
+        val = rowsum(jnp.where(only_x, box_st[g, tp], collect(ST, g)))
+        post(SX, g, colsum(pick(row8 == lane8, val)))
 
     def factors(g):
-        tot = rowsum(jnp.where(no_x, box_sx[g, x], collect(SX, g)))
+        val = jnp.where(lane_of((1, LN)) >= 3 * LG, box_sx[g, x], collect(SX, g))
+        tot = rowsum(pick(row8 == lane8, val))
         isin = row_of((2 * LG, 1)) < LG
         mean_r = tot[2 * LG:] / jnp.where(isin, NI, NOUT)
         rms = jnp.sqrt(mean_r * tot[:2 * LG] / jnp.where(isin, NI * KIN, NOUT * KO))
@@ -477,7 +490,6 @@
             local(gbuf.at[l], gbuf.at[l], gl_sem.at[NG + l]).wait()
             swap_first(l).wait_recv()
             stage_a(l)
-            step1(l).start()
             if l == 0:
                 both(swap_start, 1)
         both(lambda l: step3(l).start(), 0)
@@ -590,8 +602,10 @@
     unpack_pair(6, base)
     take_pair(6)
     for ref, sem in ((pbuf, gs_sem), (msend, ms_sem), (mall.at[first(6)], s_sem), (mall.at[first(6)], ags_sem), (mall.at[first(8)], shs_sem),
-                     (lraw.at[0], os_sem), (mt.at[first(3)], sts_sem), (lvnew, vs_sem)):
+                     (lraw.at[0], os_sem), (mt.at[first(4), first(88)], sts_sem), (lvnew, vs_sem)):
         remote(ref, ref, sem.at[0], os_sem.at[1], partner).wait_send()
+    last = box_sx.at[:, first(RING - 1)]
+    remote(last, last, sts_sem.at[1], os_sem.at[1], partner).wait_send()
 
 
 def update_call(scalars, arrays):
@@ -607,9 +621,9 @@
         lanes(LC, CH), lanes(D), lanes(NG, LN), lanes(NG, 8),
         vmem((2, 2, LC, B48), F32), vmem((LC, KI), F32), vmem((LC, NO), F32), lanes(3, 2, LC),
         lanes(NG, 8), lanes(NG, 8), lanes(2, NG, 8), lanes(2, NG, 8),
-        lanes(NG, RING, 8), lanes(NG, RING, 8), lanes(NG, TP, 8), lanes(NG, TP, 8),
+        lanes(NG, RING, 8), lanes(NG, RING, 1), lanes(NG, TP, 8), lanes(NG, TP, 8),
         dma((NG + LG,)), dma((LG,)), dma((1,)), dma((NG + LG,)), dma((2,)), dma((1,)), dma((NG,)), dma((1,)), dma((LC,)), dma((NG,)),
-        dma((1,)), dma((LC + NG + 1 + LG,)), dma((1,)), dma((NG + 1,)), dma((1,)), dma((NG, len(KINDS))), dma((1,)), dma((2,)), dma((4,)),
+        dma((1,)), dma((LC + NG + 1 + LG,)), dma((1,)), dma((NG + 1,)), dma((2,)), dma((NG, len(KINDS))), dma((1,)), dma((2,)), dma((4,)),
         dma((2,)), dma((2,)), pltpu.SemaphoreType.REGULAR,
     ]
     outs = [((L, KI, D), F32), ((L, NO, D), F32), ((L, B48, KI), BF16), ((L, B48, NO), BF16),

time: 78.3 us -> 77.8 us (level)
  no operation moved by 1% of the time
where the time goes in v5:
time: 77.8 us; the launch traced here: 77.7 us
  Pallas kernels  75.1 us (97%)
  between operations  2.58 us (3%)
    pallas_call x1, Pallas kernels, update_call(): pl.pallas_call(kernel, out_shape=[vmem(*out) for out in outs], in_specs=[...  71.9 us
    pallas_call x1, Pallas kernels, store_call(): pl.pallas_call(store_kernel, out_shape=[jax.ShapeDtypeStruct(val.shape, v...  3.21 us

profile of v5, /device:TPU:1, one launch (start us, length us, event | category | flops | bytes accessed | tf_op | source)
XLA Modules:
  0.0 77.7 jit_solution(11488334165824715855)
XLA Ops:
  2.6 71.9 %adafactor.1 = (f32[16,168,384]{2,1,0:T(8,128)S(1)}, f32[16,120,384]{2,1,0:T(8,128)S(1)}, bf16[16,48,168]{2,1,0:T(8,128)(2,1)S(1)}, bf16[16,48,120]{2,1,0:T(8,12...) custom-call(f32[1]{0:T(128)} %bitcast.11.rate_ref, ...), custom_call_target="tpu_custom_call" | custom-call | tf_op jit(solution)/shard_map/adafactor/pallas_call | solution.py:631
  74.5 3.2 %store.1 = (f32[16,168,384]{2,1,0:T(8,128)}, f32[16,120,384]{2,1,0:T(8,128)}, bf16[16,48,168]{2,1,0:T(8,128)(2,1)}, bf16[16,48,120]{2,1,0:T(8,128)(2,1)}, f32[16...) custom-call(f32[16,168,384]{2,1,0:T(8,128)S(1)} %get-tuple-element.24.refs_0_, ...), custom_call_target="tpu_custom_call" | custom-call | tf_op jit(solution)/shard_map/store/pallas_call | solution.py:653

commit v6 on v5

--- a/solution.py
+++ b/solution.py
@@ -14,7 +14,7 @@
 Q, LN, B48, B96 = 72, 128, 48, 96
 CH, HEAD, MID, HALF = 3 * Q, KI - 2 * Q, 256, 104
 NI, KIN, NOUT, KO = 384.0, 2688.0, 1920.0, 384.0
-KINDS = RV, SX, LT, ST = range(4)
+KINDS = RV, LT, SX, ST = range(4)
 TP = RING * RING
 
 
@@ -69,7 +69,7 @@
            gbuf, pbuf, gsend, pack, via, rin, fin, mall, mraw_in, mraw_out, msend, mt, mpack, tall,
            rvacc, lvacc, lraw, craw, oraw, pads, lvold, rvold, lvnew, rvnew, box_rv, box_sx, box_lt, box_st,
            gl_sem, gp_sem, gs_sem, gr_sem, ml_sem, ms_sem, mr_sem, s_sem, via_sem, rin_sem, ags_sem, agr_sem,
-           shs_sem, shr_sem, sts_sem, str_sem, vs_sem, vr_sem, ol_sem, os_sem, wl_sem, ready):
+           shs_sem, shr_sem, sts_sem, str_sem, vs_sem, ol_sem, os_sem, wl_sem, ready):
     tp, dp = lax.axis_index('tp'), lax.axis_index('dp')
     z, y, x, c = tp // RING, tp % RING, dp // 2, dp % 2
     other = 1 - c
@@ -102,7 +102,7 @@
 
     def own(l, i):
         src, dst = ((g_in, first(KI)), (g_out, pl.ds(KI, NO)))[i]
-        return local(src.at[base + l], gbuf.at[l, dst], gl_sem.at[NG + l] if isinstance(l, int) else gl_sem.at[l // LG])
+        return local(src.at[base + l], gbuf.at[l, dst], gl_sem.at[l if isinstance(l, int) else LG])
 
     def others(l, i):
         src, dst = ((g_in, first(KI)), (g_out, pl.ds(KI, NO)))[i]
@@ -164,7 +164,7 @@
     across = (x + 2) % RING
 
     def step1(l):
-        return remote(pack.at[l, across], via.at[l], s_sem.at[0], via_sem.at[l], at_x(ahead(l)))
+        return remote(pack.at[l, across], via.at[l], s_sem.at[0], via_sem.at[l // LG], at_x(ahead(l)))
 
     def step2(l):
         return remote(pack.at[l, ahead(l)], rin.at[l, 0], s_sem.at[0], rin_sem.at[l // LG], at_x(ahead(l)))
@@ -176,7 +176,7 @@
         return pl.ds(pl.multiple_of(core * B48, 16), B48)
 
     def moment_swap(l, core):
-        return remote(msend.at[l], mt.at[l, m_rows(core)], ms_sem.at[0], mr_sem.at[l // LG], partner)
+        return remote(msend.at[l], mt.at[l, m_rows(core)], ms_sem.at[0], mr_sem.at[0], partner)
 
     def stage_a(l):
         def tile(t, q):
@@ -214,7 +214,6 @@
         mt[l, m_rows(c), pl.ds(MID, NO)] = mraw_out[base + l].astype(F32)
 
     def stage_b(l):
-        step1(l).wait_recv()
         to = ahead(l)
         pack[l, to] = pack[l, to] + via[l]
         step2(l).start()
@@ -256,15 +255,16 @@
 
         def send(k, carry):
             device = at_x(me + k) if num == RING else {'tp': (me + k) % TP}
-            remote(box.at[g, me], box.at[g, me], sts_sem.at[int(kind == SX)], str_sem.at[g, kind], device).start()
+            remote(box.at[g, me], box.at[g, me], sts_sem.at[int(kind == SX)], str_sem.at[g, max(kind - 1, 0)], device).start()
             return carry
 
         lax.fori_loop(1, num, send, 0)
 
     def collect(kind, g):
         box, me, num = boxes[kind]
-        rest = box.at[g, first(num - 1)]
-        remote(rest, rest, sts_sem.at[int(kind == SX)], str_sem.at[g, kind], partner).wait_recv()
+        rest = mt.at[0, first(B48)] if kind == LT else box.at[g, first(num - 1)]
+        if kind != RV:
+            remote(rest, rest, sts_sem.at[int(kind == SX)], str_sem.at[g, max(kind - 1, 0)], partner).wait_recv()
         val = box[g, 0]
         for k in range(1, num):
             val = val + box[g, k]
@@ -296,7 +296,7 @@
 
     def vec_swap(g, half, i):
         ref = (lvnew, rvnew)[i]
-        return remote(ref.at[half, g], ref.at[half, g], vs_sem.at[0], vr_sem.at[i], partner)
+        return remote(ref.at[half, g], ref.at[half, g], vs_sem.at[0], vs_sem.at[1], partner)
 
     def moments(g):
         lv_mean = collect(LT, g) / jnp.where(row8 < LG, KIN, NOUT)
@@ -351,7 +351,7 @@
             mall[base + l, x, block(i), :] = new.astype(BF16).astype(F32)
 
     def arrived(l, k):
-        return l if k == 0 else LC + NG if k == 1 and l >= LC - LG else LC + l // LG
+        return l // LG if k == 0 else 2 * NG if k == 1 and l >= LC - LG else NG + l // LG
 
     def gather(l, k):
         slot = x if k < 2 else behind(l)
@@ -360,7 +360,7 @@
 
     def share(l, k, start):
         ref = mall.at[start + l, (behind(l), ahead(l), across, x)[k]]
-        return remote(ref, ref, shs_sem.at[0], shr_sem.at[NG if k == 3 and l >= LC - LG else l // LG], partner)
+        return remote(ref, ref, shs_sem.at[0], shr_sem.at[NG if k == 3 and l >= LC - LG else min(l // LG, NG - 1) if l < LC - 1 else NG + 1], partner)
 
     def send_pair(l):
         gather(l, 0).start()
@@ -373,17 +373,19 @@
         share(l + 1, 3, base).start()
 
     def forward_pair(l):
+        two = mall.at[base + l, first(LG)]
+        remote(two, two, ags_sem.at[0], agr_sem.at[arrived(l, 0)], partner).wait_recv()
         for k in (l, l + 1):
-            gather(k, 0).wait_recv()
             gather(k, 2).start()
             share(k, 0, base).start()
 
-    def half(ref, h):
-        return ref.at[(first(HALF), pl.ds(HALF, CH - HALF))[h]]
+    def half(ref, h, lead=0):
+        rows = (first(HALF), pl.ds(HALF, CH - HALF))[h]
+        return ref.at[:, rows] if lead else ref.at[rows]
 
     def gather_half(l, h, slot):
         ref = half(mall.at[base + l, slot], h)
-        return remote(ref, ref, ags_sem.at[0], agr_sem.at[l if h == 0 else LC + NG + 1 + l], at_x(ahead(l)))
+        return remote(ref, ref, ags_sem.at[0], agr_sem.at[0 if h == 0 else 2 * NG + 1], at_x(ahead(l)))
 
     def send_first():
         for h in range(2):
@@ -392,8 +394,9 @@
 
     def forward_first():
         for h in range(2):
+            two = half(mall.at[base, first(LG)], h, 1)
+            remote(two, two, ags_sem.at[0], agr_sem.at[0 if h == 0 else 2 * NG + 1], partner).wait_recv()
             for l in range(LG):
-                gather_half(l, h, behind(l)).wait_recv()
                 ref = half(mall.at[base + l, behind(l)], h)
                 remote(ref, ref, ags_sem.at[0], agr_sem.at[arrived(l, 2)], at_x(ahead(l))).start()
         share(0, 0, base).start()
@@ -401,7 +404,7 @@
 
     def settle_pair(l):
         four = mall.at[base + l]
-        remote(four, four, ags_sem.at[0], agr_sem.at[LC + l // LG], partner).wait_recv()
+        remote(four, four, ags_sem.at[0], agr_sem.at[arrived(0, 1) + l // LG], partner).wait_recv()
         for k in (l, l + 1):
             for i in (1, 2):
                 share(k, i, base).start()
@@ -460,9 +463,15 @@
         each(turn_moment, l, pbase)
 
     def take_pair(l):
-        two = mall.at[pl.ds(pbase + l, LG)] if l < LC - LG else mall.at[pl.ds(pbase + l, LG), first(3)]
+        two = mall.at[pl.ds(pbase + l, LG)]
         remote(two, two, shs_sem.at[0], shr_sem.at[l // LG], partner).wait_recv()
         unpack_pair(l, pbase)
+
+    def take_last():
+        for l in range(LC - LG, LC):
+            three = mall.at[pbase + l, first(3)]
+            remote(three, three, shs_sem.at[0], shr_sem.at[NG - 1 if l < LC - 1 else NG + 1], partner).wait_recv()
+            lax.fori_loop(pbase + l, pbase + l + 1, lambda at, carry: (unpack(at), carry)[1], 0)
 
     def new_vectors():
         lane4 = lane_of((LG, LN))
@@ -487,7 +496,7 @@
 
     def pack_first():
         for l in range(LG):
-            local(gbuf.at[l], gbuf.at[l], gl_sem.at[NG + l]).wait()
+            local(gbuf.at[l], gbuf.at[l], gl_sem.at[l]).wait()
             swap_first(l).wait_recv()
             stage_a(l)
             if l == 0:
@@ -496,7 +505,9 @@
 
     def pack_pair(g):
         two = pl.ds(LG * g, LG)
-        local(gbuf.at[two], gbuf.at[two], gl_sem.at[g]).wait()
+        if g == 1:
+            rest = gbuf.at[pl.ds(LG, LC - LG)]
+            local(rest, rest, gl_sem.at[LG]).wait()
         remote(pbuf.at[two], pbuf.at[two], gs_sem.at[0], gr_sem.at[g], partner).wait_recv()
         if g + 1 < NG:
             both(swap_start, g + 1)
@@ -506,13 +517,14 @@
     def direct_pair(g):
         both(lambda l: step3(l).start(), g)
 
-    def cast_pair(g):
-        if g == 0:
-            loads[0].wait()
-            loads[1].wait()
-        both(stage_n, g)
+    def cast_all():
+        loads[0].wait()
+        loads[1].wait()
+        lax.fori_loop(0, LC, lambda l, carry: (stage_n(l), carry)[1], 0)
 
     def relay_pair(g):
+        two = via.at[pl.ds(LG * g, LG)]
+        remote(two, two, s_sem.at[0], via_sem.at[g], partner).wait_recv()
         both(stage_b, g)
 
     def sum_pair(g):
@@ -522,8 +534,8 @@
         sums_send(g)
 
     def moment_pair(g):
-        two = msend.at[pl.ds(LG * g, LG)]
-        remote(two, two, ms_sem.at[0], mr_sem.at[g], partner).wait_recv()
+        if g == 0:
+            remote(msend, msend, ms_sem.at[0], mr_sem.at[0], partner).wait_recv()
         both(stage_m, g)
 
     def update_pair(g):
@@ -532,26 +544,23 @@
             update(LG * g + lg, lg, fac)
 
     pack_first()
-    cast_pair(0)
     pack_pair(1)
+    cast_all()
     w_loads[0].start()
     w_loads[1].start()
     old_vectors()
     pl.semaphore_wait(ready, RING - 1)
     relay_pair(0)
     direct_pair(1)
-    cast_pair(1)
     pack_pair(2)
     sum_pair(0)
     relay_pair(1)
     direct_pair(2)
-    cast_pair(2)
     moment_pair(0)
     pack_pair(3)
     moments(0)
     sum_pair(1)
     relay_pair(2)
-    cast_pair(3)
     moment_pair(1)
     totals(0)
     direct_pair(3)
@@ -589,8 +598,7 @@
     send_back(6)
     unpack_pair(2, base)
     take_pair(2)
-    for i, ref in enumerate((lvnew, rvnew)):
-        remote(ref.at[other], ref.at[other], vs_sem.at[0], vr_sem.at[i], partner).wait_recv()
+    remote(lvnew, lvnew, vs_sem.at[0], vs_sem.at[1], partner).wait_recv()
     new_vectors()
     turn_last()
     forward_pair(6)
@@ -600,7 +608,7 @@
     take_pair(4)
     settle_last(2)
     unpack_pair(6, base)
-    take_pair(6)
+    take_last()
     for ref, sem in ((pbuf, gs_sem), (msend, ms_sem), (mall.at[first(6)], s_sem), (mall.at[first(6)], ags_sem), (mall.at[first(8)], shs_sem),
                      (lraw.at[0], os_sem), (mt.at[first(4), first(88)], sts_sem), (lvnew, vs_sem)):
         remote(ref, ref, sem.at[0], os_sem.at[1], partner).wait_send()
@@ -622,8 +630,8 @@
         vmem((2, 2, LC, B48), F32), vmem((LC, KI), F32), vmem((LC, NO), F32), lanes(3, 2, LC),
         lanes(NG, 8), lanes(NG, 8), lanes(2, NG, 8), lanes(2, NG, 8),
         lanes(NG, RING, 8), lanes(NG, RING, 1), lanes(NG, TP, 8), lanes(NG, TP, 8),
-        dma((NG + LG,)), dma((LG,)), dma((1,)), dma((NG + LG,)), dma((2,)), dma((1,)), dma((NG,)), dma((1,)), dma((LC,)), dma((NG,)),
-        dma((1,)), dma((LC + NG + 1 + LG,)), dma((1,)), dma((NG + 1,)), dma((2,)), dma((NG, len(KINDS))), dma((1,)), dma((2,)), dma((4,)),
+        dma((LG + 1,)), dma((LG,)), dma((1,)), dma((NG + LG,)), dma((2,)), dma((1,)), dma((1,)), dma((1,)), dma((NG,)), dma((NG,)),
+        dma((1,)), dma((2 * NG + 2,)), dma((1,)), dma((NG + 2,)), dma((2,)), dma((NG, 3)), dma((2,)), dma((4,)),
         dma((2,)), dma((2,)), pltpu.SemaphoreType.REGULAR,
     ]
     outs = [((L, KI, D), F32), ((L, NO, D), F32), ((L, B48, KI), BF16), ((L, B48, NO), BF16),

time: 77.8 us -> 77.5 us (level)
  no operation moved by 1% of the time
where the time goes in v6:
time: 77.5 us; the launch traced here: 77.4 us
  Pallas kernels  74.8 us (97%)
  between operations  2.58 us (3%)
    pallas_call x1, Pallas kernels, update_call(): pl.pallas_call(kernel, out_shape=[vmem(*out) for out in outs], in_specs=[...  71.6 us
    pallas_call x1, Pallas kernels, store_call(): pl.pallas_call(store_kernel, out_shape=[jax.ShapeDtypeStruct(val.shape, v...  3.21 us

profile of v6, /device:TPU:1, one launch (start us, length us, event | category | flops | bytes accessed | tf_op | source)
XLA Modules:
  0.0 77.4 jit_solution(15014748389186682504)
XLA Ops:
  2.6 71.6 %adafactor.1 = (f32[16,168,384]{2,1,0:T(8,128)S(1)}, f32[16,120,384]{2,1,0:T(8,128)S(1)}, bf16[16,48,168]{2,1,0:T(8,128)(2,1)S(1)}, bf16[16,48,120]{2,1,0:T(8,12...) custom-call(f32[1]{0:T(128)} %bitcast.11.rate_ref, ...), custom_call_target="tpu_custom_call" | custom-call | tf_op jit(solution)/shard_map/adafactor/pallas_call | solution.py:639
  74.2 3.2 %store.1 = (f32[16,168,384]{2,1,0:T(8,128)}, f32[16,120,384]{2,1,0:T(8,128)}, bf16[16,48,168]{2,1,0:T(8,128)(2,1)}, bf16[16,48,120]{2,1,0:T(8,128)(2,1)}, f32[16...) custom-call(f32[16,168,384]{2,1,0:T(8,128)S(1)} %get-tuple-element.24.refs_0_, ...), custom_call_target="tpu_custom_call" | custom-call | tf_op jit(solution)/shard_map/store/pallas_call | solution.py:661

commit v7 on v6

--- a/solution.py
+++ b/solution.py
@@ -93,10 +93,16 @@
         return pltpu.make_async_remote_copy(src_ref=src, dst_ref=dst, send_sem=send_sem, recv_sem=recv_sem,
                                             device_id=device, device_id_type=MESH)
 
+    def greet(step):
+        for peer in plane:
+            pl.semaphore_signal(ready.at[step], inc=1, device_id=peer, device_id_type=MESH)
+
+    def greeted(step):
+        pl.semaphore_wait(ready.at[step], len(plane))
+
     barrier = pltpu.get_barrier_semaphore()
-    peers = [partner]
-    for k in range(1, RING):
-        peers += [at_x(x + k), at_y(y + k), at_z(z + k)]
+    plane = [at_y(y + 1), at_y(y + RING - 1), at_z(z + 1), at_z(z + RING - 1)]
+    peers = [partner, at_x(x + 1), at_x(x + RING - 1)] + plane
     for peer in peers:
         pl.semaphore_signal(barrier, inc=1, device_id=peer, device_id_type=MESH)
 
@@ -137,8 +143,7 @@
     for copy in loads:
         copy.start()
     pl.semaphore_wait(barrier, len(peers))
-    for k in range(1, RING):
-        pl.semaphore_signal(ready, inc=1, device_id=at_y(y + k), device_id_type=MESH)
+    greet(0)
     for l in range(LG):
         local(gsend.at[l], gsend.at[l], gp_sem.at[l]).wait()
         swap_first(l).start()
@@ -549,10 +554,14 @@
     w_loads[0].start()
     w_loads[1].start()
     old_vectors()
-    pl.semaphore_wait(ready, RING - 1)
+    greeted(0)
+    greet(1)
     relay_pair(0)
     direct_pair(1)
+    greeted(1)
+    greet(2)
     pack_pair(2)
+    greeted(2)
     sum_pair(0)
     relay_pair(1)
     direct_pair(2)
@@ -632,7 +641,7 @@
         lanes(NG, RING, 8), lanes(NG, RING, 1), lanes(NG, TP, 8), lanes(NG, TP, 8),
         dma((LG + 1,)), dma((LG,)), dma((1,)), dma((NG + LG,)), dma((2,)), dma((1,)), dma((1,)), dma((1,)), dma((NG,)), dma((NG,)),
         dma((1,)), dma((2 * NG + 2,)), dma((1,)), dma((NG + 2,)), dma((2,)), dma((NG, 3)), dma((2,)), dma((4,)),
-        dma((2,)), dma((2,)), pltpu.SemaphoreType.REGULAR,
+        dma((2,)), dma((2,)), pltpu.SemaphoreType.REGULAR((3,)),
     ]
     outs = [((L, KI, D), F32), ((L, NO, D), F32), ((L, B48, KI), BF16), ((L, B48, NO), BF16),
             ((L, B48), F32), ((L, KI), F32), ((L, NO), F32), ((L, B48), F32)]

time: 77.5 us -> 77.3 us (level)
  no operation moved by 1% of the time
where the time goes in v7:
time: 77.3 us; the launch traced here: 77.1 us
  Pallas kernels  74.6 us (97%)
  between operations  2.58 us (3%)
    pallas_call x1, Pallas kernels, update_call(): pl.pallas_call(kernel, out_shape=[vmem(*out) for out in outs], in_specs=[...  71.4 us
    pallas_call x1, Pallas kernels, store_call(): pl.pallas_call(store_kernel, out_shape=[jax.ShapeDtypeStruct(val.shape, v...  3.21 us

profile of v7, /device:TPU:1, one launch (start us, length us, event | category | flops | bytes accessed | tf_op | source)
XLA Modules:
  0.0 77.1 jit_solution(10747316019069488103)
XLA Ops:
  2.6 71.4 %adafactor.1 = (f32[16,168,384]{2,1,0:T(8,128)S(1)}, f32[16,120,384]{2,1,0:T(8,128)S(1)}, bf16[16,48,168]{2,1,0:T(8,128)(2,1)S(1)}, bf16[16,48,120]{2,1,0:T(8,12...) custom-call(f32[1]{0:T(128)} %bitcast.11.rate_ref, ...), custom_call_target="tpu_custom_call" | custom-call | tf_op jit(solution)/shard_map/adafactor/pallas_call | solution.py:648
  73.9 3.2 %store.1 = (f32[16,168,384]{2,1,0:T(8,128)}, f32[16,120,384]{2,1,0:T(8,128)}, bf16[16,48,168]{2,1,0:T(8,128)(2,1)}, bf16[16,48,120]{2,1,0:T(8,128)(2,1)}, f32[16...) custom-call(f32[16,168,384]{2,1,0:T(8,128)S(1)} %get-tuple-element.24.refs_0_, ...), custom_call_target="tpu_custom_call" | custom-call | tf_op jit(solution)/shard_map/store/pallas_call | solution.py:670

commit v8 on v7

--- a/solution.py
+++ b/solution.py
@@ -658,11 +658,14 @@
 
 def store_kernel(*refs):
     num = len(refs) // 2
-    copies = [pltpu.make_async_copy(src, dst, refs[-1].at[i]) for i, (src, dst) in enumerate(zip(refs[:num], refs[num:-1]))]
-    for copy in copies:
-        copy.start()
-    for copy in copies:
-        copy.wait()
+    pairs = list(zip(refs[:num], refs[num:-1]))
+    for i, (src, dst) in enumerate(pairs):
+        step = LG * 2 if i < 2 else L
+        for l in range(0, L, step):
+            part = pl.ds(l, step)
+            pltpu.make_async_copy(src.at[part], dst.at[part], refs[-1].at[i]).start(priority=(l // step) % 2)
+    for i, (src, dst) in enumerate(pairs):
+        pltpu.make_async_copy(src, dst, refs[-1].at[i]).wait()
 
 
 def store_call(vals):

time: 77.3 us -> 77.3 us (level)
  no operation moved by 1% of the time
where the time goes in v8:
time: 77.3 us; the launch traced here: 77.1 us
  Pallas kernels  74.5 us (96%)
  between operations  2.58 us (3%)
    pallas_call x1, Pallas kernels, update_call(): pl.pallas_call(kernel, out_shape=[vmem(*out) for out in outs], in_specs=[...  71.4 us
    pallas_call x1, Pallas kernels, store_call(): pl.pallas_call(store_kernel, out_shape=[jax.ShapeDtypeStruct(val.shape, v...  3.19 us

profile of v8, /device:TPU:1, one launch (start us, length us, event | category | flops | bytes accessed | tf_op | source)
XLA Modules:
  0.0 77.1 jit_solution(12675463916501552638)
XLA Ops:
  2.6 71.4 %adafactor.1 = (f32[16,168,384]{2,1,0:T(8,128)S(1)}, f32[16,120,384]{2,1,0:T(8,128)S(1)}, bf16[16,48,168]{2,1,0:T(8,128)(2,1)S(1)}, bf16[16,48,120]{2,1,0:T(8,12...) custom-call(f32[1]{0:T(128)} %bitcast.11.rate_ref, ...), custom_call_target="tpu_custom_call" | custom-call | tf_op jit(solution)/shard_map/adafactor/pallas_call | solution.py:648
  73.9 3.2 %store.1 = (f32[16,168,384]{2,1,0:T(8,128)}, f32[16,120,384]{2,1,0:T(8,128)}, bf16[16,48,168]{2,1,0:T(8,128)(2,1)}, bf16[16,48,120]{2,1,0:T(8,128)(2,1)}, f32[16...) custom-call(f32[16,168,384]{2,1,0:T(8,128)S(1)} %get-tuple-element.24.refs_0_, ...), custom_call_target="tpu_custom_call" | custom-call | tf_op jit(solution)/shard_map/store/pallas_call | solution.py:673
